TPU v7x, 32 devices: a whole 2x2x4 slice. The times are simulated.
32 devices in a mesh: dp: 2 (over x), tp: 4 (over z), pp: 4 (over y, core).
Axes of the slice: x: 2, y: 2, z: 4, core: 2. Of those that a mesh axis runs over, the one named last changes fastest.
Arguments:
- hidden_in: bfloat16 [512, 2560], P('dp'), parts along dimension 0
- positions: int32 [512], P('dp'), parts along dimension 0
- k_cache: bfloat16 [4, 512, 32, 8, 128], P('pp', 'dp', None, 'tp'), parts along dimension 1
- v_cache: bfloat16 [4, 512, 32, 8, 128], P('pp', 'dp', None, 'tp'), parts along dimension 1
- attn_gain: bfloat16 [4, 2560], P('pp')
- w_q: bfloat16 [4, 2560, 4096], P('pp', None, 'tp')
- w_k: bfloat16 [4, 2560, 1024], P('pp', None, 'tp')
- w_v: bfloat16 [4, 2560, 1024], P('pp', None, 'tp')
- w_o: bfloat16 [4, 4096, 2560], P('pp', 'tp')
- mlp_gain: bfloat16 [4, 2560], P('pp')
- w_gate: bfloat16 [4, 2560, 9728], P('pp', None, 'tp')
- w_up: bfloat16 [4, 2560, 9728], P('pp', None, 'tp')
- w_down: bfloat16 [4, 9728, 2560], P('pp', 'tp')
- final_gain: bfloat16 [2560], replicated
Outputs:
- output 1: bfloat16 [512, 2560], P('dp'), parts along dimension 0
- output 2: bfloat16 [4, 512, 8, 128], P('pp', 'dp', 'tp'), parts along dimension 1
- output 3: bfloat16 [4, 512, 8, 128], P('pp', 'dp', 'tp'), parts along dimension 1
There are 2 independent parts. A program takes and returns all parts, laid end to end along the dimension named above; an argument that names none is the same for every part.
All inputs are finite; a program needn't handle non-finite values.
Results may differ from a plain program's by a relative error of at most 0.02.
Values are sent between devices in bfloat16 or wider.
A program may use at most 1 GiB of HBM per device.

v0:
```python
import jax
import jax.numpy as jnp
from jax import lax
from jax.sharding import PartitionSpec as P

RMS_EPS = 1e-5
ROPE_THETA = 500000.0


def rms_norm(hidden, gain_vec):
    hidden32 = hidden.astype(jnp.float32)
    mean_sq = jnp.mean(hidden32 * hidden32, axis=-1, keepdims=True)
    return (hidden32 * lax.rsqrt(mean_sq + RMS_EPS) * gain_vec.astype(jnp.float32)).astype(jnp.bfloat16)


def rope_tables(positions, head_dim):
    freq_idx = jnp.arange(0, head_dim, 2).astype(jnp.float32)
    inv_freq = ROPE_THETA ** (-freq_idx / head_dim)
    angles = positions.astype(jnp.float32)[:, None] * inv_freq[None, :]
    return jnp.cos(angles), jnp.sin(angles)


def apply_rope(head_vals, cos_t, sin_t):
    half_dim = head_vals.shape[-1] // 2
    heads32 = head_vals.astype(jnp.float32)
    first_half = heads32[..., :half_dim]
    second_half = heads32[..., half_dim:]
    cos_b = cos_t[:, None, :]
    sin_b = sin_t[:, None, :]
    return jnp.concatenate([first_half * cos_b - second_half * sin_b, second_half * cos_b + first_half * sin_b], axis=-1).astype(jnp.bfloat16)


def layer_fwd(hidden, cos_t, sin_t, cache_mask, k_layer, v_layer, gain_attn, q_weight, k_weight, v_weight, o_weight, gain_mlp, gate_weight, up_weight, down_weight):
    row_count = hidden.shape[0]
    kv_local = k_layer.shape[2]
    head_dim = k_layer.shape[3]
    normed = rms_norm(hidden, gain_attn)
    queries = jnp.dot(normed, q_weight, preferred_element_type=jnp.float32).astype(jnp.bfloat16)
    queries = apply_rope(queries.reshape(row_count, -1, head_dim), cos_t, sin_t).reshape(row_count, kv_local, -1, head_dim)
    keys_new = jnp.dot(normed, k_weight, preferred_element_type=jnp.float32).astype(jnp.bfloat16)
    keys_new = apply_rope(keys_new.reshape(row_count, kv_local, head_dim), cos_t, sin_t)
    vals_new = jnp.dot(normed, v_weight, preferred_element_type=jnp.float32).astype(jnp.bfloat16).reshape(row_count, kv_local, head_dim)
    score_scale = head_dim ** -0.5
    scores = jnp.einsum('sgrh,stgh->sgrt', queries, k_layer, preferred_element_type=jnp.float32) * score_scale
    score_new = jnp.einsum('sgrh,sgh->sgr', queries, keys_new, preferred_element_type=jnp.float32) * score_scale
    scores = jnp.where(cache_mask[:, None, None, :], scores, -jnp.inf)
    top_score = jnp.maximum(jnp.max(scores, axis=-1), score_new)
    exp_scores = jnp.exp(scores - top_score[..., None])
    exp_new = jnp.exp(score_new - top_score)
    denominator = jnp.sum(exp_scores, axis=-1) + exp_new
    prob_cache = (exp_scores / denominator[..., None]).astype(jnp.bfloat16)
    prob_new = (exp_new / denominator).astype(jnp.bfloat16)
    context = jnp.einsum('sgrt,stgh->sgrh', prob_cache, v_layer, preferred_element_type=jnp.float32)
    context = context + prob_new.astype(jnp.float32)[..., None] * vals_new.astype(jnp.float32)[:, :, None, :]
    context = context.astype(jnp.bfloat16).reshape(row_count, -1)
    attn_out = lax.psum(jnp.dot(context, o_weight, preferred_element_type=jnp.float32), 'tp').astype(jnp.bfloat16)
    hidden = (hidden.astype(jnp.float32) + attn_out.astype(jnp.float32)).astype(jnp.bfloat16)
    mlp_in = rms_norm(hidden, gain_mlp)
    gate_val = jnp.dot(mlp_in, gate_weight, preferred_element_type=jnp.float32).astype(jnp.bfloat16)
    up_val = jnp.dot(mlp_in, up_weight, preferred_element_type=jnp.float32).astype(jnp.bfloat16)
    act_val = (jax.nn.silu(gate_val.astype(jnp.float32)) * up_val.astype(jnp.float32)).astype(jnp.bfloat16)
    mlp_out = lax.psum(jnp.dot(act_val, down_weight, preferred_element_type=jnp.float32), 'tp').astype(jnp.bfloat16)
    hidden = (hidden.astype(jnp.float32) + mlp_out.astype(jnp.float32)).astype(jnp.bfloat16)
    return hidden, keys_new, vals_new


def write_rows(row_buffer, new_rows, row_start, in_range):
    old_rows = lax.dynamic_slice_in_dim(row_buffer, row_start, new_rows.shape[1], 1)
    return lax.dynamic_update_slice_in_dim(row_buffer, jnp.where(in_range, new_rows, old_rows), row_start, 1)


def solution(mesh):
    n_stage = mesh.shape['pp']
    n_tp = mesh.shape['tp']
    send_pairs = [(src_stage, src_stage + 1) for src_stage in range(n_stage - 1)]
    cache_spec = P('pp', 'dp', None, 'tp', None)
    gain_spec = P('pp', None)
    col_spec = P('pp', None, 'tp')
    row_spec = P('pp', 'tp', None)
    rows_spec = P('pp', 'dp', 'tp', None)

    def stage_fn(hidden_in, positions, k_cache, v_cache, attn_gain, q_weight, k_weight, v_weight, o_weight, mlp_gain, gate_weight, up_weight, down_weight, final_gain):
        batch_rows, d_model = hidden_in.shape
        group_rows = batch_rows // n_stage
        n_layers = q_weight.shape[0]
        cache_len = k_cache.shape[2]
        kv_local = k_cache.shape[3]
        head_dim = k_cache.shape[4]
        part_width = d_model // n_tp
        stage_idx = lax.axis_index('pp')
        tp_rank = lax.axis_index('tp')

        def tick(tick_idx, loop_state):
            carried, k_rows, v_rows, out_buf = loop_state
            group_idx = tick_idx - stage_idx
            in_range = (group_idx >= 0) & (group_idx < n_stage)
            row_start = jnp.clip(group_idx, 0, n_stage - 1) * group_rows
            fresh_rows = lax.dynamic_slice_in_dim(hidden_in, row_start, group_rows, 0)
            hidden = jnp.where(stage_idx == 0, fresh_rows, carried)
            group_pos = lax.dynamic_slice_in_dim(positions, row_start, group_rows, 0)
            cos_t, sin_t = rope_tables(group_pos, head_dim)
            cache_mask = jnp.arange(cache_len)[None, :] < group_pos[:, None]
            k_list = []
            v_list = []
            for layer_idx in range(n_layers):
                k_layer = lax.dynamic_slice_in_dim(k_cache[layer_idx], row_start, group_rows, 0)
                v_layer = lax.dynamic_slice_in_dim(v_cache[layer_idx], row_start, group_rows, 0)
                hidden, k_row, v_row = layer_fwd(hidden, cos_t, sin_t, cache_mask, k_layer, v_layer, attn_gain[layer_idx], q_weight[layer_idx], k_weight[layer_idx], v_weight[layer_idx], o_weight[layer_idx], mlp_gain[layer_idx], gate_weight[layer_idx], up_weight[layer_idx], down_weight[layer_idx])
                k_list.append(k_row)
                v_list.append(v_row)
            k_rows = write_rows(k_rows, jnp.stack(k_list), row_start, in_range)
            v_rows = write_rows(v_rows, jnp.stack(v_list), row_start, in_range)
            final_rows = rms_norm(hidden, final_gain)
            keep_final = in_range & (stage_idx == n_stage - 1)
            old_out = lax.dynamic_slice_in_dim(out_buf, row_start, group_rows, 0)
            out_buf = lax.dynamic_update_slice_in_dim(out_buf, jnp.where(keep_final, final_rows, old_out), row_start, 0)
            own_part = lax.dynamic_slice_in_dim(hidden, tp_rank * part_width, part_width, 1)
            received = lax.ppermute(own_part, 'pp', send_pairs)
            carried = lax.all_gather(received, 'tp', axis=1, tiled=True)
            return carried, k_rows, v_rows, out_buf

        init_state = (
            jnp.zeros((group_rows, d_model), jnp.bfloat16),
            jnp.zeros((n_layers, batch_rows, kv_local, head_dim), jnp.bfloat16),
            jnp.zeros((n_layers, batch_rows, kv_local, head_dim), jnp.bfloat16),
            jnp.zeros((batch_rows, d_model), jnp.bfloat16),
        )
        loop_out = lax.fori_loop(0, 2 * n_stage - 1, tick, init_state)
        hidden_out = lax.psum(loop_out[3], 'pp')
        return hidden_out, loop_out[1], loop_out[2]

    return jax.shard_map(
        stage_fn,
        mesh=mesh,
        in_specs=(P('dp', None), P('dp'), cache_spec, cache_spec, gain_spec, col_spec, col_spec, col_spec, row_spec, gain_spec, col_spec, col_spec, row_spec, P(None)),
        out_specs=(P('dp', None), rows_spec, rows_spec),
        check_vma=False,
    )
```

profile of v0, /device:TPU:0, one launch (start us, length us, event | category | flops | bytes accessed | tf_op | source)
XLA Modules:
  0.0 857.9 jit_solution(6064909399137206062)
XLA Ops:
  9.8 801.4 %while.21 = (s32[]{:T(128)}, bf16[64,2560]{1,0:T(8,128)(2,1)S(1)}, bf16[1,256,2,128]{3,2,1,0:T(2,128)(2,1)}, bf16[1,256,2,128]{3,2,1,0:T(2,128)(2,1)}, bf16[256,...) while((s32[]{:T(128)}, bf16[64,2560]{1,0:T(8,128)(2,1)S(1)}, ...), condition=%wide.region_8.9_spmd, body=%wide.region_0.8_spmd.sunk | while | flops 3248604672 | bytes 81826896 | solution.py:128
  11.9 3.6 fusion.137
  16.2 3.6 constant_dynamic-slice_fusion.5
  28.2 34.6 %all-reduce.5 = bf16[64,2560]{1,0:T(8,128)(2,1)S(1)} all-reduce(f32[64,2560]{1,0:T(8,128)S(1)} %fusion.147), channel_id=1, replica_groups=mesh['dp'=2,'tp'=4,'pp'=4] {'tp'}, use_global_device_ids=true, to_apply=%region_4.4 | all-reduce | flops 163840 | bytes 983040 | tf_op jit(solution)/shard_map/while/body/eval_jaxpr/psum | solution.py:56
  63.1 6.9 fusion.149
  70.0 12.6 %fusion.150 = f32[64,2560]{1,0:T(8,128)S(1)} fusion(bf16[1,2432,2560]{2,1,0:T(8,128)(2,1)} %get-tuple-element.883, bf16[1,2560,2432]{2,1,0:T(8,128)(2,1)} %get-tuple-element.882, f32[64,2432]{1,0:T(8,128)S(1)} %fusion.149, bf16[64,2560]{1,0:T(8,128)(2,1)S(1)} %get-tuple-element.800, f32[2560]{0:T(1024)S(1)} %convert_reduce_fusion.5, ...), kind=kOutput, calls=%fused_computation.clone.1 | convolution fusion | flops 1595736064 | bytes 26519808 | tf_op jit(solution)/shard_map/while/body/eval_jaxpr/dot_general | solution.py:62
  82.6 27.5 %all-reduce.6 = bf16[64,2560]{1,0:T(8,128)(2,1)S(1)} all-reduce(f32[64,2560]{1,0:T(8,128)S(1)} %fusion.150), channel_id=1, replica_groups=mesh['dp'=2,'tp'=4,'pp'=4] {'tp'}, use_global_device_ids=true, to_apply=%region_6.6 | all-reduce | flops 163840 | bytes 983040 | tf_op jit(solution)/shard_map/while/body/eval_jaxpr/psum | solution.py:62
  115.2 14.8 %all_gather.10 = bf16[64,2560]{1,0:T(8,128)(2,1)S(1)} all-gather(bf16[64,640]{1,0:T(8,128)(2,1)S(1)} %collective-permute-done), channel_id=1, replica_groups=mesh['dp'=2,'tp'=4,'pp'=4] {'tp'}, dimensions={1}, use_global_device_ids=true | all-gather | bytes 409600 | tf_op jit(solution)/shard_map/while/body/eval_jaxpr/all_gather | solution.py:119
  132.0 3.6 fusion.137
  136.3 3.6 constant_dynamic-slice_fusion.5
  148.3 31.4 %all-reduce.5 = bf16[64,2560]{1,0:T(8,128)(2,1)S(1)} all-reduce(f32[64,2560]{1,0:T(8,128)S(1)} %fusion.147), channel_id=1, replica_groups=mesh['dp'=2,'tp'=4,'pp'=4] {'tp'}, use_global_device_ids=true, to_apply=%region_4.4 | all-reduce | flops 163840 | bytes 983040 | tf_op jit(solution)/shard_map/while/body/eval_jaxpr/psum | solution.py:56
  180.0 6.9 fusion.149
  186.9 12.6 %fusion.150 = f32[64,2560]{1,0:T(8,128)S(1)} fusion(bf16[1,2432,2560]{2,1,0:T(8,128)(2,1)} %get-tuple-element.883, bf16[1,2560,2432]{2,1,0:T(8,128)(2,1)} %get-tuple-element.882, f32[64,2432]{1,0:T(8,128)S(1)} %fusion.149, bf16[64,2560]{1,0:T(8,128)(2,1)S(1)} %get-tuple-element.800, f32[2560]{0:T(1024)S(1)} %convert_reduce_fusion.5, ...), kind=kOutput, calls=%fused_computation.clone.1 | convolution fusion | flops 1595736064 | bytes 26519808 | tf_op jit(solution)/shard_map/while/body/eval_jaxpr/dot_general | solution.py:62
  199.5 27.5 %all-reduce.6 = bf16[64,2560]{1,0:T(8,128)(2,1)S(1)} all-reduce(f32[64,2560]{1,0:T(8,128)S(1)} %fusion.150), channel_id=1, replica_groups=mesh['dp'=2,'tp'=4,'pp'=4] {'tp'}, use_global_device_ids=true, to_apply=%region_6.6 | all-reduce | flops 163840 | bytes 983040 | tf_op jit(solution)/shard_map/while/body/eval_jaxpr/psum | solution.py:62
  232.1 14.3 %all_gather.10 = bf16[64,2560]{1,0:T(8,128)(2,1)S(1)} all-gather(bf16[64,640]{1,0:T(8,128)(2,1)S(1)} %collective-permute-done), channel_id=1, replica_groups=mesh['dp'=2,'tp'=4,'pp'=4] {'tp'}, dimensions={1}, use_global_device_ids=true | all-gather | bytes 409600 | tf_op jit(solution)/shard_map/while/body/eval_jaxpr/all_gather | solution.py:119
  252.7 3.6 constant_dynamic-slice_fusion.5
  264.8 27.4 %all-reduce.5 = bf16[64,2560]{1,0:T(8,128)(2,1)S(1)} all-reduce(f32[64,2560]{1,0:T(8,128)S(1)} %fusion.147), channel_id=1, replica_groups=mesh['dp'=2,'tp'=4,'pp'=4] {'tp'}, use_global_device_ids=true, to_apply=%region_4.4 | all-reduce | flops 163840 | bytes 983040 | tf_op jit(solution)/shard_map/while/body/eval_jaxpr/psum | solution.py:56
  292.5 6.9 fusion.149
  299.4 12.6 %fusion.150 = f32[64,2560]{1,0:T(8,128)S(1)} fusion(bf16[1,2432,2560]{2,1,0:T(8,128)(2,1)} %get-tuple-element.883, bf16[1,2560,2432]{2,1,0:T(8,128)(2,1)} %get-tuple-element.882, f32[64,2432]{1,0:T(8,128)S(1)} %fusion.149, bf16[64,2560]{1,0:T(8,128)(2,1)S(1)} %get-tuple-element.800, f32[2560]{0:T(1024)S(1)} %convert_reduce_fusion.5, ...), kind=kOutput, calls=%fused_computation.clone.1 | convolution fusion | flops 1595736064 | bytes 26519808 | tf_op jit(solution)/shard_map/while/body/eval_jaxpr/dot_general | solution.py:62
  311.9 27.6 %all-reduce.6 = bf16[64,2560]{1,0:T(8,128)(2,1)S(1)} all-reduce(f32[64,2560]{1,0:T(8,128)S(1)} %fusion.150), channel_id=1, replica_groups=mesh['dp'=2,'tp'=4,'pp'=4] {'tp'}, use_global_device_ids=true, to_apply=%region_6.6 | all-reduce | flops 163840 | bytes 983040 | tf_op jit(solution)/shard_map/while/body/eval_jaxpr/psum | solution.py:62
  344.6 14.7 %all_gather.10 = bf16[64,2560]{1,0:T(8,128)(2,1)S(1)} all-gather(bf16[64,640]{1,0:T(8,128)(2,1)S(1)} %collective-permute-done), channel_id=1, replica_groups=mesh['dp'=2,'tp'=4,'pp'=4] {'tp'}, dimensions={1}, use_global_device_ids=true | all-gather | bytes 409600 | tf_op jit(solution)/shard_map/while/body/eval_jaxpr/all_gather | solution.py:119
  361.4 3.6 fusion.137
  365.6 3.6 constant_dynamic-slice_fusion.5
  377.7 27.9 %all-reduce.5 = bf16[64,2560]{1,0:T(8,128)(2,1)S(1)} all-reduce(f32[64,2560]{1,0:T(8,128)S(1)} %fusion.147), channel_id=1, replica_groups=mesh['dp'=2,'tp'=4,'pp'=4] {'tp'}, use_global_device_ids=true, to_apply=%region_4.4 | all-reduce | flops 163840 | bytes 983040 | tf_op jit(solution)/shard_map/while/body/eval_jaxpr/psum | solution.py:56
  405.9 6.9 fusion.149
  412.8 12.6 %fusion.150 = f32[64,2560]{1,0:T(8,128)S(1)} fusion(bf16[1,2432,2560]{2,1,0:T(8,128)(2,1)} %get-tuple-element.883, bf16[1,2560,2432]{2,1,0:T(8,128)(2,1)} %get-tuple-element.882, f32[64,2432]{1,0:T(8,128)S(1)} %fusion.149, bf16[64,2560]{1,0:T(8,128)(2,1)S(1)} %get-tuple-element.800, f32[2560]{0:T(1024)S(1)} %convert_reduce_fusion.5, ...), kind=kOutput, calls=%fused_computation.clone.1 | convolution fusion | flops 1595736064 | bytes 26519808 | tf_op jit(solution)/shard_map/while/body/eval_jaxpr/dot_general | solution.py:62
  425.4 28.3 %all-reduce.6 = bf16[64,2560]{1,0:T(8,128)(2,1)S(1)} all-reduce(f32[64,2560]{1,0:T(8,128)S(1)} %fusion.150), channel_id=1, replica_groups=mesh['dp'=2,'tp'=4,'pp'=4] {'tp'}, use_global_device_ids=true, to_apply=%region_6.6 | all-reduce | flops 163840 | bytes 983040 | tf_op jit(solution)/shard_map/while/body/eval_jaxpr/psum | solution.py:62
  458.7 14.0 %all_gather.10 = bf16[64,2560]{1,0:T(8,128)(2,1)S(1)} all-gather(bf16[64,640]{1,0:T(8,128)(2,1)S(1)} %collective-permute-done), channel_id=1, replica_groups=mesh['dp'=2,'tp'=4,'pp'=4] {'tp'}, dimensions={1}, use_global_device_ids=true | all-gather | bytes 409600 | tf_op jit(solution)/shard_map/while/body/eval_jaxpr/all_gather | solution.py:119
  474.8 3.6 fusion.137
  479.1 3.6 constant_dynamic-slice_fusion.5
  491.1 27.9 %all-reduce.5 = bf16[64,2560]{1,0:T(8,128)(2,1)S(1)} all-reduce(f32[64,2560]{1,0:T(8,128)S(1)} %fusion.147), channel_id=1, replica_groups=mesh['dp'=2,'tp'=4,'pp'=4] {'tp'}, use_global_device_ids=true, to_apply=%region_4.4 | all-reduce | flops 163840 | bytes 983040 | tf_op jit(solution)/shard_map/while/body/eval_jaxpr/psum | solution.py:56
  519.2 6.9 fusion.149
  526.1 12.6 %fusion.150 = f32[64,2560]{1,0:T(8,128)S(1)} fusion(bf16[1,2432,2560]{2,1,0:T(8,128)(2,1)} %get-tuple-element.883, bf16[1,2560,2432]{2,1,0:T(8,128)(2,1)} %get-tuple-element.882, f32[64,2432]{1,0:T(8,128)S(1)} %fusion.149, bf16[64,2560]{1,0:T(8,128)(2,1)S(1)} %get-tuple-element.800, f32[2560]{0:T(1024)S(1)} %convert_reduce_fusion.5, ...), kind=kOutput, calls=%fused_computation.clone.1 | convolution fusion | flops 1595736064 | bytes 26519808 | tf_op jit(solution)/shard_map/while/body/eval_jaxpr/dot_general | solution.py:62
  538.7 28.4 %all-reduce.6 = bf16[64,2560]{1,0:T(8,128)(2,1)S(1)} all-reduce(f32[64,2560]{1,0:T(8,128)S(1)} %fusion.150), channel_id=1, replica_groups=mesh['dp'=2,'tp'=4,'pp'=4] {'tp'}, use_global_device_ids=true, to_apply=%region_6.6 | all-reduce | flops 163840 | bytes 983040 | tf_op jit(solution)/shard_map/while/body/eval_jaxpr/psum | solution.py:62
  572.2 14.0 %all_gather.10 = bf16[64,2560]{1,0:T(8,128)(2,1)S(1)} all-gather(bf16[64,640]{1,0:T(8,128)(2,1)S(1)} %collective-permute-done), channel_id=1, replica_groups=mesh['dp'=2,'tp'=4,'pp'=4] {'tp'}, dimensions={1}, use_global_device_ids=true | all-gather | bytes 409600 | tf_op jit(solution)/shard_map/while/body/eval_jaxpr/all_gather | solution.py:119
  592.6 3.6 constant_dynamic-slice_fusion.5
  604.6 27.1 %all-reduce.5 = bf16[64,2560]{1,0:T(8,128)(2,1)S(1)} all-reduce(f32[64,2560]{1,0:T(8,128)S(1)} %fusion.147), channel_id=1, replica_groups=mesh['dp'=2,'tp'=4,'pp'=4] {'tp'}, use_global_device_ids=true, to_apply=%region_4.4 | all-reduce | flops 163840 | bytes 983040 | tf_op jit(solution)/shard_map/while/body/eval_jaxpr/psum | solution.py:56
  632.0 6.9 fusion.149
  638.9 12.6 %fusion.150 = f32[64,2560]{1,0:T(8,128)S(1)} fusion(bf16[1,2432,2560]{2,1,0:T(8,128)(2,1)} %get-tuple-element.883, bf16[1,2560,2432]{2,1,0:T(8,128)(2,1)} %get-tuple-element.882, f32[64,2432]{1,0:T(8,128)S(1)} %fusion.149, bf16[64,2560]{1,0:T(8,128)(2,1)S(1)} %get-tuple-element.800, f32[2560]{0:T(1024)S(1)} %convert_reduce_fusion.5, ...), kind=kOutput, calls=%fused_computation.clone.1 | convolution fusion | flops 1595736064 | bytes 26519808 | tf_op jit(solution)/shard_map/while/body/eval_jaxpr/dot_general | solution.py:62
  651.4 28.5 %all-reduce.6 = bf16[64,2560]{1,0:T(8,128)(2,1)S(1)} all-reduce(f32[64,2560]{1,0:T(8,128)S(1)} %fusion.150), channel_id=1, replica_groups=mesh['dp'=2,'tp'=4,'pp'=4] {'tp'}, use_global_device_ids=true, to_apply=%region_6.6 | all-reduce | flops 163840 | bytes 983040 | tf_op jit(solution)/shard_map/while/body/eval_jaxpr/psum | solution.py:62
  685.0 14.0 %all_gather.10 = bf16[64,2560]{1,0:T(8,128)(2,1)S(1)} all-gather(bf16[64,640]{1,0:T(8,128)(2,1)S(1)} %collective-permute-done), channel_id=1, replica_groups=mesh['dp'=2,'tp'=4,'pp'=4] {'tp'}, dimensions={1}, use_global_device_ids=true | all-gather | bytes 409600 | tf_op jit(solution)/shard_map/while/body/eval_jaxpr/all_gather | solution.py:119
  705.4 3.6 constant_dynamic-slice_fusion.5
  717.4 26.6 %all-reduce.5 = bf16[64,2560]{1,0:T(8,128)(2,1)S(1)} all-reduce(f32[64,2560]{1,0:T(8,128)S(1)} %fusion.147), channel_id=1, replica_groups=mesh['dp'=2,'tp'=4,'pp'=4] {'tp'}, use_global_device_ids=true, to_apply=%region_4.4 | all-reduce | flops 163840 | bytes 983040 | tf_op jit(solution)/shard_map/while/body/eval_jaxpr/psum | solution.py:56
  744.3 6.9 fusion.149
  751.2 12.6 %fusion.150 = f32[64,2560]{1,0:T(8,128)S(1)} fusion(bf16[1,2432,2560]{2,1,0:T(8,128)(2,1)} %get-tuple-element.883, bf16[1,2560,2432]{2,1,0:T(8,128)(2,1)} %get-tuple-element.882, f32[64,2432]{1,0:T(8,128)S(1)} %fusion.149, bf16[64,2560]{1,0:T(8,128)(2,1)S(1)} %get-tuple-element.800, f32[2560]{0:T(1024)S(1)} %convert_reduce_fusion.5, ...), kind=kOutput, calls=%fused_computation.clone.1 | convolution fusion | flops 1595736064 | bytes 26519808 | tf_op jit(solution)/shard_map/while/body/eval_jaxpr/dot_general | solution.py:62
  763.8 27.5 %all-reduce.6 = bf16[64,2560]{1,0:T(8,128)(2,1)S(1)} all-reduce(f32[64,2560]{1,0:T(8,128)S(1)} %fusion.150), channel_id=1, replica_groups=mesh['dp'=2,'tp'=4,'pp'=4] {'tp'}, use_global_device_ids=true, to_apply=%region_6.6 | all-reduce | flops 163840 | bytes 983040 | tf_op jit(solution)/shard_map/while/body/eval_jaxpr/psum | solution.py:62
  796.4 14.8 %all_gather.10 = bf16[64,2560]{1,0:T(8,128)(2,1)S(1)} all-gather(bf16[64,640]{1,0:T(8,128)(2,1)S(1)} %collective-permute-done), channel_id=1, replica_groups=mesh['dp'=2,'tp'=4,'pp'=4] {'tp'}, dimensions={1}, use_global_device_ids=true | all-gather | bytes 409600 | tf_op jit(solution)/shard_map/while/body/eval_jaxpr/all_gather | solution.py:119
  811.2 37.4 %all-reduce.4.cloned.1.call-done = bf16[256,2560]{1,0:T(8,128)(2,1)} async-done(((bf16[256,2560]{1,0:T(8,128)(2,1)}), bf16[256,2560]{1,0:T(8,128)(2,1)}) %all-reduce.4.cloned.1.call-update) | async-done | bytes 1310736 | tf_op jit(solution)/shard_map/psum | solution.py:129
  (381 shorter events, 129.9 us)
Async XLA Ops:
  7.2 841.5 %all-reduce.4.cloned.1.call-start = ((), (), s32[]{:S(2)}) async-start(), calls=%async_computation | async-start | bytes 2621440 | tf_op jit(solution)/shard_map/psum | solution.py:129
  9.8 5.7 copy-start.5
  9.8 5.9 copy-start.1
  15.7 5.4 copy-start
  20.1 0.9 copy-start.2
  24.6 38.4 %copy-start.3 = (bf16[1,2560]{1,0:T(2,128)(2,1)S(1)}, bf16[1,2560]{1,0:T(2,128)(2,1)}, u32[]{:S(2)}) copy-start(bf16[1,2560]{1,0:T(2,128)(2,1)} %get-tuple-element.880) | copy-start | bytes 15364 | tf_op jit(solution)/shard_map/while
  70.0 41.7 %copy-start.4 = (bf16[2560]{0:T(1024)(128)(2,1)S(1)}, bf16[2560]{0:T(1024)(128)(2,1)}, u32[]{:S(2)}) copy-start(bf16[2560]{0:T(1024)(128)(2,1)} %get-tuple-element.886) | copy-start | bytes 15364 | tf_op jit(solution)/shard_map/while
  110.4 4.8 collective-permute-start
  130.0 5.7 copy-start.5
  130.0 5.9 copy-start.1
  135.8 5.4 copy-start
  140.2 0.9 copy-start.2
  144.7 35.2 %copy-start.3 = (bf16[1,2560]{1,0:T(2,128)(2,1)S(1)}, bf16[1,2560]{1,0:T(2,128)(2,1)}, u32[]{:S(2)}) copy-start(bf16[1,2560]{1,0:T(2,128)(2,1)} %get-tuple-element.880) | copy-start | bytes 15364 | tf_op jit(solution)/shard_map/while
  186.9 41.7 %copy-start.4 = (bf16[2560]{0:T(1024)(128)(2,1)S(1)}, bf16[2560]{0:T(1024)(128)(2,1)}, u32[]{:S(2)}) copy-start(bf16[2560]{0:T(1024)(128)(2,1)} %get-tuple-element.886) | copy-start | bytes 15364 | tf_op jit(solution)/shard_map/while
  227.3 4.8 collective-permute-start
  246.4 5.7 copy-start.5
  246.4 5.9 copy-start.1
  252.3 5.4 copy-start
  256.7 0.9 copy-start.2
  261.2 31.2 %copy-start.3 = (bf16[1,2560]{1,0:T(2,128)(2,1)S(1)}, bf16[1,2560]{1,0:T(2,128)(2,1)}, u32[]{:S(2)}) copy-start(bf16[1,2560]{1,0:T(2,128)(2,1)} %get-tuple-element.880) | copy-start | bytes 15364 | tf_op jit(solution)/shard_map/while
  299.3 41.8 %copy-start.4 = (bf16[2560]{0:T(1024)(128)(2,1)S(1)}, bf16[2560]{0:T(1024)(128)(2,1)}, u32[]{:S(2)}) copy-start(bf16[2560]{0:T(1024)(128)(2,1)} %get-tuple-element.886) | copy-start | bytes 15364 | tf_op jit(solution)/shard_map/while
  339.8 4.8 collective-permute-start
  359.3 5.7 copy-start.5
  359.3 5.9 copy-start.1
  365.2 5.4 copy-start
  369.6 0.9 copy-start.2
  374.1 31.8 %copy-start.3 = (bf16[1,2560]{1,0:T(2,128)(2,1)S(1)}, bf16[1,2560]{1,0:T(2,128)(2,1)}, u32[]{:S(2)}) copy-start(bf16[1,2560]{1,0:T(2,128)(2,1)} %get-tuple-element.880) | copy-start | bytes 15364 | tf_op jit(solution)/shard_map/while
  412.8 42.4 %copy-start.4 = (bf16[2560]{0:T(1024)(128)(2,1)S(1)}, bf16[2560]{0:T(1024)(128)(2,1)}, u32[]{:S(2)}) copy-start(bf16[2560]{0:T(1024)(128)(2,1)} %get-tuple-element.886) | copy-start | bytes 15364 | tf_op jit(solution)/shard_map/while
  453.9 4.8 collective-permute-start
  472.7 5.7 copy-start.5
  472.7 5.9 copy-start.1
  478.6 5.4 copy-start
  483.0 0.9 copy-start.2
  487.5 31.7 %copy-start.3 = (bf16[1,2560]{1,0:T(2,128)(2,1)S(1)}, bf16[1,2560]{1,0:T(2,128)(2,1)}, u32[]{:S(2)}) copy-start(bf16[1,2560]{1,0:T(2,128)(2,1)} %get-tuple-element.880) | copy-start | bytes 15364 | tf_op jit(solution)/shard_map/while
  526.1 42.6 %copy-start.4 = (bf16[2560]{0:T(1024)(128)(2,1)S(1)}, bf16[2560]{0:T(1024)(128)(2,1)}, u32[]{:S(2)}) copy-start(bf16[2560]{0:T(1024)(128)(2,1)} %get-tuple-element.886) | copy-start | bytes 15364 | tf_op jit(solution)/shard_map/while
  567.4 4.8 collective-permute-start
  586.2 5.7 copy-start.5
  586.2 5.9 copy-start.1
  592.1 5.4 copy-start
  601.0 30.9 %copy-start.3 = (bf16[1,2560]{1,0:T(2,128)(2,1)S(1)}, bf16[1,2560]{1,0:T(2,128)(2,1)}, u32[]{:S(2)}) copy-start(bf16[1,2560]{1,0:T(2,128)(2,1)} %get-tuple-element.880) | copy-start | bytes 15364 | tf_op jit(solution)/shard_map/while
  638.9 42.7 %copy-start.4 = (bf16[2560]{0:T(1024)(128)(2,1)S(1)}, bf16[2560]{0:T(1024)(128)(2,1)}, u32[]{:S(2)}) copy-start(bf16[2560]{0:T(1024)(128)(2,1)} %get-tuple-element.886) | copy-start | bytes 15364 | tf_op jit(solution)/shard_map/while
  680.2 4.8 collective-permute-start
  699.0 5.7 copy-start.5
  699.0 5.9 copy-start.1
  704.9 5.4 copy-start
  713.8 30.5 %copy-start.3 = (bf16[1,2560]{1,0:T(2,128)(2,1)S(1)}, bf16[1,2560]{1,0:T(2,128)(2,1)}, u32[]{:S(2)}) copy-start(bf16[1,2560]{1,0:T(2,128)(2,1)} %get-tuple-element.880) | copy-start | bytes 15364 | tf_op jit(solution)/shard_map/while
  751.2 41.7 %copy-start.4 = (bf16[2560]{0:T(1024)(128)(2,1)S(1)}, bf16[2560]{0:T(1024)(128)(2,1)}, u32[]{:S(2)}) copy-start(bf16[2560]{0:T(1024)(128)(2,1)} %get-tuple-element.886) | copy-start | bytes 15364 | tf_op jit(solution)/shard_map/while
  791.6 4.8 collective-permute-start
  (2 other events, 1.8 us)
Sparse Core Ops, SparseCore 0:
  811.4 37.2 all-reduce.3
where the time goes:
time: 860 us; the launch traced here: 858 us
  blocking collectives  499 us (58%)
  matrix products  209 us (24%)
  other arithmetic  50.5 us (6%)
  waiting for transfers between devices  37.4 us (4%)
  local copies, waits for them, and re-layouts  36.2 us (4%)
  between operations  14 us (2%)
  starting transfers between devices  9.1 us (1%)
    psum x7, blocking collectives, layer_fwd(): lax.psum(jnp.dot(context, o_weight, preferred_element_type=jnp.float32),...  203 us
    psum x7, blocking collectives, layer_fwd(): lax.psum(jnp.dot(act_val, down_weight, preferred_element_type=jnp.float32...  195 us
    all_gather x7, blocking collectives, tick(): carried = lax.all_gather(received, 'tp', axis=1, tiled=True)  101 us
    dot_general x7, matrix products, layer_fwd(): jnp.dot(act_val, down_weight, preferred_element_type=jnp.float32)  88 us
    dot_general x7, matrix products, layer_fwd(): jnp.dot(mlp_in, gate_weight, preferred_element_type=jnp.float32)  48 us
    psum x1, waiting for transfers between devices, stage_fn(): hidden_out = lax.psum(loop_out[3], 'pp')  37.4 us
    dynamic_slice x7, local copies, waits for them, and re-layouts, tick(): lax.dynamic_slice_in_dim(v_cache[layer_idx], row_start, group_rows, 0)  25 us
    dot_general x7, matrix products, layer_fwd(): jnp.dot(normed, q_weight, preferred_element_type=jnp.float32)  24.9 us
  transfers between devices with their start and end apart: 8, of which 1 were waited for; matrix products, arithmetic and copies ran while one was open for 3% of the time, Pallas kernels for 0%

commit v1 on v0

v1 whole, which is shorter than its diff:
```python
import functools

import jax
import jax.numpy as jnp
from jax import lax
from jax.experimental import pallas as pl
from jax.experimental.pallas import tpu as pltpu
from jax.sharding import PartitionSpec as P

RMS_EPS = 1e-5
ROPE_THETA = 500000.0
BF16 = jnp.bfloat16
F32 = jnp.float32
MESH = pl.DeviceIdType.MESH

N_CHUNK = 4
N_SUB = 5
GROUP = 16


def rope_tables(positions, head_dim):
    freq_idx = jnp.arange(0, head_dim, 2).astype(F32)
    inv_freq = ROPE_THETA ** (-freq_idx / head_dim)
    angles = positions.astype(F32)[:, None] * inv_freq[None, :]
    return jnp.cos(angles), jnp.sin(angles)


def norm_rows(rows, gain):
    rows32 = rows.astype(F32)
    mean_sq = jnp.mean(rows32 * rows32, axis=-1, keepdims=True)
    return (rows32 * lax.rsqrt(mean_sq + RMS_EPS) * gain.astype(F32)).astype(BF16)


def dot(a, b):
    return jnp.dot(a, b, preferred_element_type=F32)


def column_blocks(width, size):
    return [(at, min(size, width - at)) for at in range(0, width, size)]


def step_kernel(
    n_stage, n_tp,
    hid, pos, cos_t, sin_t, k_hbm, v_hbm, gain_a, w_q, w_k, w_v, w_o, gain_m, w_g, w_u, w_d, gain_f,
    out, k_out, v_out,
    wq, wk, wv, wg, wu, wd, kb, vb, hb, nb, qb, kn, vn, cb, ab, slots,
    part, rec_e, rec_m, res_a, res_b, hrec0, hrec1, hrec_m, hres,
    s_w, s_kv, s_rows, s_out, s_fwd,
    r_h, s_h, r_out, s_part, s_sum, s_res, r_e, r_m, r_a, r_b,
    s_hsum, s_hres0, s_hres1, r_h0, r_h1, r_hm,
):
    rows = hb.shape[1]
    sub = part.shape[3]
    half = N_SUB * sub
    d_attn = cb.shape[1]
    kv_width = kn.shape[2]
    head_dim = kb.shape[2]
    n_head = d_attn // head_dim
    kv_heads = kv_width // head_dim
    per_kv = n_head // kv_heads
    cache_len = kb.shape[1] // (rows * kv_heads)
    stage = lax.axis_index('pp')
    line = lax.axis_index('tp')
    side = stage // 2
    helped = lax.rem(stage + 2, n_stage)
    is_mid = jnp.logical_or(line == 1, line == n_tp - 2)
    is_end = jnp.logical_not(is_mid)
    mid_of = jnp.where(line < n_tp // 2, 1, n_tp - 2)
    end_of = jnp.where(line < n_tp // 2, 0, n_tp - 1)
    other_mid = n_tp - 1 - line

    def remote(src, dst, send, recv, to_stage, to_line):
        return pltpu.make_async_remote_copy(
            src_ref=src, dst_ref=dst, send_sem=send, recv_sem=recv,
            device_id={'pp': to_stage, 'tp': to_line}, device_id_type=MESH)

    def landed(ref, sem):
        pltpu.make_async_copy(ref, ref, sem).wait()

    barrier = pltpu.get_barrier_semaphore()
    for other_stage in range(n_stage):
        for other_line in range(n_tp):
            pl.semaphore_signal(barrier, inc=1, device_id={'pp': other_stage, 'tp': other_line}, device_id_type=MESH)

    @pl.when(stage == 0)
    def _():
        for c in range(N_CHUNK):
            pltpu.make_async_copy(hid.at[c], hb.at[c], r_h.at[c]).start()

    def load_kv(c, slot):
        return (pltpu.make_async_copy(k_hbm.at[c], kb.at[slot], s_kv.at[0, slot]),
                pltpu.make_async_copy(v_hbm.at[c], vb.at[slot], s_kv.at[1, slot]))

    o_rows = w_o.shape[0]
    loads = [
        pltpu.make_async_copy(w_q, wq, s_w.at[0]),
        pltpu.make_async_copy(w_k, wk, s_w.at[1]),
        pltpu.make_async_copy(w_v, wv, s_w.at[2]),
        pltpu.make_async_copy(w_o, wd.at[pl.ds(0, o_rows)], s_w.at[3]),
        pltpu.make_async_copy(w_g, wg, s_w.at[4]),
        pltpu.make_async_copy(w_u, wu, s_w.at[5]),
        pltpu.make_async_copy(w_d.at[pl.ds(o_rows, w_d.shape[0] - o_rows)], wd.at[pl.ds(o_rows, w_d.shape[0] - o_rows)], s_w.at[6]),
        pltpu.make_async_copy(w_d.at[pl.ds(0, o_rows)], wd.at[pl.ds(0, o_rows)], s_w.at[7]),
    ]
    for one in loads[:3]:
        one.start()
    for one in load_kv(0, 0):
        one.start()
    loads[3].start()

    @pl.when(stage > 0)
    def _():
        for one in loads[4:7]:
            one.start()
        pl.semaphore_wait(barrier, n_stage * n_tp)

    row_id = lax.broadcasted_iota(jnp.int32, slots.shape, 0)
    col_id = lax.broadcasted_iota(jnp.int32, slots.shape, 1)
    keys_per_row = cache_len * kv_heads
    quad = slots.shape[1] // keys_per_row
    same_row = lax.rem(row_id, quad) == col_id // keys_per_row
    same_head = lax.rem(col_id, kv_heads) == row_id // (GROUP * per_kv)
    slots[...] = jnp.where(jnp.logical_and(same_row, same_head), lax.rem(col_id, keys_per_row) // kv_heads, cache_len)

    def send_part(k, b_half):
        kc = lax.rem(k, N_CHUNK)
        base = N_SUB if b_half else 0
        if b_half:
            @pl.when(is_end)
            def _():
                for s in range(N_SUB):
                    remote(part.at[kc, base + s], hrec0.at[kc, s], s_part.at[kc, base + s], r_h0.at[kc, s], helped, mid_of).start()

            @pl.when(is_mid)
            def _():
                for s in range(N_SUB):
                    remote(part.at[kc, base + s], hrec1.at[kc, s], s_part.at[kc, base + s], r_h1.at[kc, s], helped, line).start()
        else:
            @pl.when(is_end)
            def _():
                for s in range(N_SUB):
                    remote(part.at[kc, s], rec_e.at[kc, s], s_part.at[kc, s], r_e.at[kc, s], stage, mid_of).start()

    def wait_part_sends(k):
        kc = lax.rem(k, N_CHUNK)
        for s in range(N_SUB):
            landed(part.at[kc, N_SUB + s], s_part.at[kc, N_SUB + s])

        @pl.when(is_end)
        def _():
            for s in range(N_SUB):
                landed(part.at[kc, s], s_part.at[kc, s])

        @pl.when(is_mid)
        def _():
            for s in range(N_SUB):
                landed(part.at[kc, s], s_sum.at[kc, s])

    def sum_first(k):
        kc = lax.rem(k, N_CHUNK)
        for s in range(N_SUB):
            landed(rec_e.at[kc, s], r_e.at[kc, s])
            part[kc, s] = part[kc, s] + rec_e[kc, s]
            remote(part.at[kc, s], rec_m.at[k, s], s_sum.at[kc, s], r_m.at[k, s], stage, other_mid).start()

    def sum_second(k):
        kc = lax.rem(k, N_CHUNK)

        @pl.when(k >= N_CHUNK)
        def _():
            for s in range(N_SUB):
                landed(res_a.at[kc, s], s_res.at[kc, s])

        for s in range(N_SUB):
            landed(rec_m.at[k, s], r_m.at[k, s])
            res_a[kc, s] = (part[kc, s] + rec_m[k, s]).astype(BF16)
            remote(res_a.at[kc, s], res_a.at[kc, s], s_res.at[kc, s], r_a.at[kc, s], stage, end_of).start()

    def help_first(k):
        kc = lax.rem(k, N_CHUNK)
        for s in range(N_SUB):
            landed(hrec0.at[kc, s], r_h0.at[kc, s])
            landed(hrec1.at[kc, s], r_h1.at[kc, s])
            hrec1[kc, s] = hrec1[kc, s] + hrec0[kc, s]
            remote(hrec1.at[kc, s], hrec_m.at[k, s], s_hsum.at[kc, s], r_hm.at[k, s], stage, other_mid).start()

    def help_second(k):
        kc = lax.rem(k, N_CHUNK)

        @pl.when(k >= N_CHUNK)
        def _():
            for s in range(N_SUB):
                landed(hres.at[kc, s], s_hres0.at[kc, s])
                landed(hres.at[kc, s], s_hres1.at[kc, s])

        for s in range(N_SUB):
            landed(hrec_m.at[k, s], r_hm.at[k, s])
            landed(hrec1.at[kc, s], s_hsum.at[kc, s])
            hres[kc, s] = (hrec1[kc, s] + hrec_m[k, s]).astype(BF16)
            remote(hres.at[kc, s], res_b.at[kc, s], s_hres0.at[kc, s], r_b.at[kc, s], helped, end_of).start()
            remote(hres.at[kc, s], res_b.at[kc, s], s_hres1.at[kc, s], r_b.at[kc, s], helped, line).start()

    def help_stage():
        @pl.when(is_mid)
        def _():
            @pl.loop(0, 2 * N_CHUNK + 1)
            def _(k):
                @pl.when(k < 2 * N_CHUNK)
                def _():
                    help_first(k)

                @pl.when(k >= 1)
                def _():
                    help_second(k - 1)

    def relay(k):
        @pl.when(is_mid)
        def _():
            @pl.when(jnp.logical_and(k >= 1, k <= 2 * N_CHUNK))
            def _():
                sum_first(k - 1)

            @pl.when(jnp.logical_and(k >= 2, k <= 2 * N_CHUNK + 1))
            def _():
                sum_second(k - 2)

    def add_sum(c):
        @pl.when(is_end)
        def _():
            for s in range(N_SUB):
                landed(res_a.at[c, s], r_a.at[c, s])

        for s in range(N_SUB):
            at = pl.ds(s * sub, sub)
            hb[c, :, at] = (hb[c, :, at].astype(F32) + res_a[c, s].astype(F32)).astype(BF16)
        for s in range(N_SUB):
            at = pl.ds(half + s * sub, sub)
            landed(res_b.at[c, s], r_b.at[c, s])
            hb[c, :, at] = (hb[c, :, at].astype(F32) + res_b[c, s].astype(F32)).astype(BF16)

    def partials(k, act, weight, depth):
        kc = lax.rem(k, N_CHUNK)
        for b_half in (True, False):
            base = N_SUB if b_half else 0
            got = dot(act, weight[pl.ds(0, depth), pl.ds(half if b_half else 0, half)])
            for s in range(N_SUB):
                part[kc, base + s] = got[:, s * sub:(s + 1) * sub]
            send_part(k, b_half)

    def attention(c):
        slot = lax.rem(c, 2)
        landed(hb.at[c], r_h.at[c])

        @pl.when(c == 0)
        def _():
            for one in loads[:3]:
                one.wait()

        normed = norm_rows(hb[c], gain_a[...])
        base = pl.multiple_of(c * rows, rows)
        cosv = cos_t[pl.ds(base, rows), :]
        sinv = sin_t[pl.ds(base, rows), :]

        def rope(vals):
            vals32 = vals.astype(BF16).astype(F32)
            return (vals32 * cosv + pltpu.roll(vals32, head_dim // 2, 1) * sinv).astype(BF16)

        nb[...] = normed
        got_k = dot(nb[...], wk[...])
        got_v = dot(nb[...], wv[...])
        for g in range(kv_heads):
            at = pl.ds(g * head_dim, head_dim)
            kn[c, :, at] = rope(got_k[:, g * head_dim:(g + 1) * head_dim])
        vn[c] = got_v.astype(BF16)
        pltpu.make_async_copy(kn.at[c], k_out.at[c], s_rows.at[0, c]).start()
        pltpu.make_async_copy(vn.at[c], v_out.at[c], s_rows.at[1, c]).start()
        got_q = dot(nb[...], wq[...])
        for h in range(n_head):
            qb[:, pl.ds(h * head_dim, head_dim)] = rope(got_q[:, h * head_dim:(h + 1) * head_dim])

        for one in load_kv(c, slot):
            one.wait()
        scale = head_dim ** -0.5
        keys = slots.shape[1]
        n_quad = GROUP // quad
        rows_id = lax.broadcasted_iota(jnp.int32, (GROUP * n_head, keys), 0)
        quad_of = lax.rem(rows_id, GROUP) // quad
        slot_of = slots[...]
        groups = range(rows // GROUP)
        queries = []
        scores = []
        for g in groups:
            rows_at = pl.ds(g * GROUP, GROUP)
            queries.append(jnp.concatenate([qb[rows_at, pl.ds(h * head_dim, head_dim)] for h in range(n_head)], axis=0))
            picked = None
            for j in range(n_quad):
                key_block = kb[slot, pl.ds(g * GROUP * keys_per_row + j * keys, keys), :]
                one = lax.dot_general(queries[g], key_block, (((1,), (1,)), ((), ())), preferred_element_type=F32)
                picked = one if picked is None else jnp.where(quad_of == j, one, picked)
            scores.append(picked * scale)
        probs = []
        probs_new = []
        values_new = []
        for g in groups:
            rows_at = pl.ds(g * GROUP, GROUP)
            key_new = jnp.concatenate([kn[c, rows_at, pl.ds((h // per_kv) * head_dim, head_dim)] for h in range(n_head)], axis=0)
            values_new.append(jnp.concatenate([vn[c, rows_at, pl.ds((h // per_kv) * head_dim, head_dim)] for h in range(n_head)], axis=0))
            score_new = jnp.sum(queries[g].astype(F32) * key_new.astype(F32), axis=-1, keepdims=True) * scale
            p_rows = pos[pl.ds(pl.multiple_of(base + g * GROUP, GROUP), GROUP), :]
            p_wide = jnp.concatenate([jnp.concatenate([p_rows] * (keys // p_rows.shape[1]), axis=1)] * n_head, axis=0)
            valid = slot_of < p_wide
            masked = jnp.where(valid, scores[g], -jnp.inf)
            top = jnp.maximum(jnp.max(masked, axis=-1, keepdims=True), score_new)
            exps = jnp.exp(masked - top)
            exp_new = jnp.exp(score_new - top)
            total = jnp.sum(exps, axis=-1, keepdims=True) + exp_new
            probs.append(exps / total)
            probs_new.append((exp_new / total).astype(BF16).astype(F32))
        for g in groups:
            context = None
            for j in range(n_quad):
                val_block = vb[slot, pl.ds(g * GROUP * keys_per_row + j * keys, keys), :]
                one = dot(jnp.where(quad_of == j, probs[g], 0.0).astype(BF16), val_block)
                context = one if context is None else context + one
            context = (context + probs_new[g] * values_new[g].astype(F32)).astype(BF16)
            for h in range(n_head):
                cb[pl.ds(g * GROUP, GROUP), pl.ds(h * head_dim, head_dim)] = context[h * GROUP:(h + 1) * GROUP]

    def attn_part(c):
        @pl.when(c + 1 < N_CHUNK)
        def _():
            for one in load_kv(c + 1, lax.rem(c + 1, 2)):
                one.start()

        attention(c)

        @pl.when(c == 0)
        def _():
            loads[3].wait()

            @pl.when(stage == 0)
            def _():
                for one in loads[4:7]:
                    one.start()
                pl.semaphore_wait(barrier, n_stage * n_tp)

        partials(c, cb[...], wd, o_rows)

        @pl.when(c == N_CHUNK - 1)
        def _():
            loads[7].start()

    def mlp_part(k):
        c = k - N_CHUNK
        add_sum(c)
        nb[...] = norm_rows(hb[c], gain_m[...])

        @pl.when(c == 0)
        def _():
            for one in loads[4:6]:
                one.wait()

        for at, size in column_blocks(wg.shape[1], 512):
            gate = dot(nb[...], wg[:, pl.ds(at, size)]).astype(BF16).astype(F32)
            up = dot(nb[...], wu[:, pl.ds(at, size)]).astype(BF16).astype(F32)
            ab[:, pl.ds(at, size)] = (gate * jax.nn.sigmoid(gate) * up).astype(BF16)

        @pl.when(c == 0)
        def _():
            for one in loads[6:]:
                one.wait()

        wait_part_sends(k - N_CHUNK)
        partials(k, ab[...], wd, wd.shape[0])

    def finish(c):
        add_sum(c)

        @pl.when(stage < n_stage - 1)
        def _():
            remote(hb.at[c], hb.at[c], s_h.at[c], r_h.at[c], stage + 1, line).start()

        @pl.when(stage == n_stage - 1)
        def _():
            hb[c] = norm_rows(hb[c], gain_f[...])
            remote(hb.at[c], out.at[c], s_fwd.at[0, c], r_out.at[c], stage - 2, line).start()
            remote(hb.at[c], out.at[c], s_fwd.at[1, c], r_out.at[c], stage - 1, line).start()
            pltpu.make_async_copy(hb.at[c], out.at[c], s_out.at[c]).start()

    def compute_stage():
        @pl.loop(0, N_CHUNK)
        def _(k):
            attn_part(k)
            relay(k)

        @pl.loop(N_CHUNK, 2 * N_CHUNK)
        def _(k):
            mlp_part(k)
            relay(k)

        @pl.loop(2 * N_CHUNK, 3 * N_CHUNK)
        def _(k):
            finish(k - 2 * N_CHUNK)
            relay(k)

    @pl.when(side == 1)
    def _():
        help_stage()

    compute_stage()

    @pl.when(side == 0)
    def _():
        help_stage()

    @pl.loop(0, N_CHUNK)
    def _(c):
        wait_part_sends(c)
        for i, (ref, dst) in enumerate(((kn, k_out), (vn, v_out))):
            landed(ref.at[c], s_rows.at[i, c])

        @pl.when(is_mid)
        def _():
            for s in range(N_SUB):
                landed(res_a.at[c, s], s_res.at[c, s])
                landed(hres.at[c, s], s_hres0.at[c, s])
                landed(hres.at[c, s], s_hres1.at[c, s])

        @pl.when(stage < n_stage - 1)
        def _():
            landed(hb.at[c], s_h.at[c])
            landed(out.at[c], r_out.at[c])

        @pl.when(stage == n_stage - 3)
        def _():
            remote(out.at[c], out.at[c], s_fwd.at[0, c], r_out.at[c], stage - 1, line).start()

        @pl.when(stage == n_stage - 1)
        def _():
            landed(hb.at[c], s_out.at[c])
            landed(hb.at[c], s_fwd.at[0, c])
            landed(hb.at[c], s_fwd.at[1, c])

    @pl.when(stage == n_stage - 3)
    def _():
        for c in range(N_CHUNK):
            landed(out.at[c], s_fwd.at[0, c])


def solution(mesh):
    n_stage = mesh.shape['pp']
    n_tp = mesh.shape['tp']
    cache_spec = P('pp', 'dp', None, 'tp', None)
    gain_spec = P('pp', None)
    col_spec = P('pp', None, 'tp')
    row_spec = P('pp', 'tp', None)
    rows_spec = P('pp', 'dp', 'tp', None)

    def stage_fn(hidden_in, positions, k_cache, v_cache, attn_gain, w_q, w_k, w_v, w_o, mlp_gain, w_gate, w_up, w_down, final_gain):
        batch, d_model = hidden_in.shape
        _, _, cache_len, kv_local, head_dim = k_cache.shape
        rows = batch // N_CHUNK
        d_attn = w_q.shape[2]
        kv_width = kv_local * head_dim
        d_ff = w_gate.shape[2]
        half = d_model // 2
        sub = half // N_SUB
        n_head = d_attn // head_dim
        keys = rows * cache_len * kv_local
        score_keys = 4 * cache_len * kv_local
        cos_h, sin_h = rope_tables(positions, head_dim)
        cos_t = jnp.concatenate([cos_h, cos_h], axis=-1)
        sin_t = jnp.concatenate([-sin_h, sin_h], axis=-1)
        pos_wide = jnp.broadcast_to(positions[:, None], (batch, 128))
        anywhere = pl.BlockSpec(memory_space=pl.ANY)
        vmem = pl.BlockSpec(memory_space=pltpu.VMEM)
        dma = pltpu.SemaphoreType.DMA
        blocks = (N_CHUNK, N_SUB)
        call = pl.pallas_call(
            functools.partial(step_kernel, n_stage, n_tp),
            out_shape=[
                jax.ShapeDtypeStruct((N_CHUNK, rows, d_model), BF16),
                jax.ShapeDtypeStruct((N_CHUNK, rows, kv_width), BF16),
                jax.ShapeDtypeStruct((N_CHUNK, rows, kv_width), BF16),
            ],
            in_specs=[anywhere, vmem, vmem, vmem, anywhere, anywhere, vmem] + [anywhere] * 4 + [vmem] + [anywhere] * 3 + [vmem],
            out_specs=[anywhere] * 3,
            scratch_shapes=[
                pltpu.VMEM((d_model, d_attn), BF16),
                pltpu.VMEM((d_model, kv_width), BF16),
                pltpu.VMEM((d_model, kv_width), BF16),
                pltpu.VMEM((d_model, d_ff), BF16),
                pltpu.VMEM((d_model, d_ff), BF16),
                pltpu.VMEM((d_ff, d_model), BF16),
                pltpu.VMEM((2, keys, head_dim), BF16),
                pltpu.VMEM((2, keys, head_dim), BF16),
                pltpu.VMEM((N_CHUNK, rows, d_model), BF16),
                pltpu.VMEM((rows, d_model), BF16),
                pltpu.VMEM((rows, d_attn), BF16),
                pltpu.VMEM((N_CHUNK, rows, kv_width), BF16),
                pltpu.VMEM((N_CHUNK, rows, kv_width), BF16),
                pltpu.VMEM((rows, d_attn), BF16),
                pltpu.VMEM((rows, d_ff), BF16),
                pltpu.VMEM((GROUP * n_head, score_keys), jnp.int32),
                pltpu.VMEM((N_CHUNK, 2 * N_SUB, rows, sub), F32),
                pltpu.VMEM(blocks + (rows, sub), F32),
                pltpu.VMEM((2 * N_CHUNK, N_SUB, rows, sub), F32),
                pltpu.VMEM(blocks + (rows, sub), BF16),
                pltpu.VMEM(blocks + (rows, sub), BF16),
                pltpu.VMEM(blocks + (rows, sub), F32),
                pltpu.VMEM(blocks + (rows, sub), F32),
                pltpu.VMEM((2 * N_CHUNK, N_SUB, rows, sub), F32),
                pltpu.VMEM(blocks + (rows, sub), BF16),
                dma((8,)), dma((2, 2)), dma((2, N_CHUNK)), dma((N_CHUNK,)), dma((2, N_CHUNK)),
                dma((N_CHUNK,)), dma((N_CHUNK,)), dma((N_CHUNK,)),
                dma((N_CHUNK, 2 * N_SUB)), dma(blocks), dma(blocks),
                dma(blocks), dma((2 * N_CHUNK, N_SUB)), dma(blocks), dma(blocks),
                dma(blocks), dma(blocks), dma(blocks), dma(blocks), dma(blocks), dma((2 * N_CHUNK, N_SUB)),
            ],
            compiler_params=pltpu.CompilerParams(collective_id=0, has_side_effects=True, vmem_limit_bytes=67043328),
        )
        out, k_rows, v_rows = call(
            hidden_in.reshape(N_CHUNK, rows, d_model), pos_wide, cos_t, sin_t,
            k_cache.reshape(N_CHUNK, keys, head_dim), v_cache.reshape(N_CHUNK, keys, head_dim),
            attn_gain, w_q[0], w_k[0], w_v[0], w_o[0], mlp_gain, w_gate[0], w_up[0], w_down[0], final_gain[None])
        shape = (1, batch, kv_local, head_dim)
        return out.reshape(batch, d_model), k_rows.reshape(shape), v_rows.reshape(shape)

    return jax.shard_map(
        stage_fn,
        mesh=mesh,
        in_specs=(P('dp', None), P('dp'), cache_spec, cache_spec, gain_spec, col_spec, col_spec, col_spec, row_spec, gain_spec, col_spec, col_spec, row_spec, P(None)),
        out_specs=(P('dp', None), rows_spec, rows_spec),
        check_vma=False,
    )
```

time: 860 us -> 281 us (0.33)
  blocking collectives: 499 us -> 0 us
  Pallas kernels: 0 us -> 269 us
  matrix products: 209 us -> 0 us
  other arithmetic: 50.5 us -> 2.06 us
  waiting for transfers between devices: 37.4 us -> 0 us
  local copies, waits for them, and re-layouts: 36.2 us -> 8.37 us
  between operations: 14 us -> 0.65 us
  starting transfers between devices: 9.1 us -> 0 us
    psum x14 -> x0, blocking collectives: 398 us -> none  [the longest x7 203 us: layer_fwd(): lax.psum(jnp.dot(context, o_weight, preferred_element_type=jnp.float32),...]
    pallas_call x0 -> x1, Pallas kernels: none -> 269 us  [stage_fn(): call(hidden_in.reshape(N_CHUNK, rows, d_model), pos_wide, cos_t, sin_t, k...]
    dot_general x63 -> x0, matrix products: 209 us -> none  [the longest x7 88 us: layer_fwd(): jnp.dot(act_val, down_weight, preferred_element_type=jnp.float32)]
    all_gather x7 -> x0, blocking collectives: 101 us -> none  [tick(): carried = lax.all_gather(received, 'tp', axis=1, tiled=True)]
    psum x1 -> x0, waiting for transfers between devices: 37.4 us -> none  [stage_fn(): hidden_out = lax.psum(loop_out[3], 'pp')]
    dynamic_slice x14 -> x0, local copies, waits for them, and re-layouts: 25.1 us -> none  [the longest x7 25 us: tick(): lax.dynamic_slice_in_dim(v_cache[layer_idx], row_start, group_rows, 0)]
    dynamic_update_slice x14 -> x0, other arithmetic: 24 us -> none  [the longest x7 13.2 us: tick(): lax.dynamic_update_slice_in_dim(out_buf, jnp.where(keep_final, final_rows...]
    reduce_sum x28 -> x0, other arithmetic: 14.4 us -> none  [the longest x21 11.5 us: rms_norm(): mean_sq = jnp.mean(hidden32 * hidden32, axis=-1, keepdims=True)]
  transfers between devices with their start and end apart: 8 -> 0, of which waited for: 1 -> 0; matrix products, arithmetic and copies ran while one was open for 3% -> 0% of each run, Pallas kernels for 0% -> 0%
where the time goes in v1:
time: 281 us; the launch traced here: 280 us
  Pallas kernels  269 us (96%)
  local copies, waits for them, and re-layouts  8.37 us (3%)
    pallas_call x1, Pallas kernels, stage_fn(): call(hidden_in.reshape(N_CHUNK, rows, d_model), pos_wide, cos_t, sin_t, k...  269 us

profile of v1, /device:TPU:0, one launch (start us, length us, event | category | flops | bytes accessed | tf_op | source)
XLA Modules:
  0.0 279.7 jit_solution(15307014137274337052)
XLA Ops:
  0.6 0.7 convert_element_type.10
  1.3 1.3 broadcast_in_dim.5.gain_f
  2.6 1.4 broadcast_in_dim.4.pos
  4.1 0.5 fusion
  4.6 0.8 pad_maximum_fusion
  5.4 268.6 %shard_map.157 = (bf16[4,64,2560]{2,1,0:T(8,128)(2,1)}, bf16[4,64,256]{2,1,0:T(8,128)(2,1)}, bf16[4,64,256]{2,1,0:T(8,128)(2,1)}) custom-call(bf16[4,64,2560]{2,1,0:T(8,128)(2,1)} %bitcast.19, s32[256,128]{1,0:T(8,128)} %broadcast_in_dim.4.pos, f32[256,128]{1,0:T(8,128)} %get-tuple-element.12.cos_t, f32[256,128]{1,0:T(8,128)} %get-tuple-element.13.sin_t, ...), custom_call_target="tpu_custom_call" | custom-call | tf_op jit(solution)/shard_map/pallas_call | solution.py:522
  274.1 1.6 reshape.38
  275.7 1.6 reshape.39
  277.3 2.5 copy.18
  (1 shorter events, 0.0 us)

commit v2 on v1

--- a/solution.py
+++ b/solution.py
@@ -129,7 +129,7 @@
             @pl.when(is_end)
             def _():
                 for s in range(N_SUB):
-                    remote(part.at[kc, base + s], hrec0.at[kc, s], s_part.at[kc, base + s], r_h0.at[kc, s], helped, mid_of).start()
+                    remote(part.at[kc, base + s], hrec_m.at[k, s], s_part.at[kc, base + s], r_hm.at[k, s], helped, line).start()
 
             @pl.when(is_mid)
             def _():
@@ -200,7 +200,25 @@
             remote(hres.at[kc, s], res_b.at[kc, s], s_hres0.at[kc, s], r_b.at[kc, s], helped, end_of).start()
             remote(hres.at[kc, s], res_b.at[kc, s], s_hres1.at[kc, s], r_b.at[kc, s], helped, line).start()
 
+    def help_forward(k):
+        kc = lax.rem(k, N_CHUNK)
+
+        @pl.when(k >= N_CHUNK)
+        def _():
+            for s in range(N_SUB):
+                landed(hrec0.at[kc, s], s_hsum.at[kc, s])
+
+        for s in range(N_SUB):
+            landed(hrec_m.at[k, s], r_hm.at[k, s])
+            remote(hrec_m.at[k, s], hrec0.at[kc, s], s_hsum.at[kc, s], r_h0.at[kc, s], stage, mid_of).start()
+
     def help_stage():
+        @pl.when(is_end)
+        def _():
+            @pl.loop(0, 2 * N_CHUNK)
+            def _(k):
+                help_forward(k)
+
         @pl.when(is_mid)
         def _():
             @pl.loop(0, 2 * N_CHUNK + 1)
@@ -425,6 +443,11 @@
                 landed(res_a.at[c, s], s_res.at[c, s])
                 landed(hres.at[c, s], s_hres0.at[c, s])
                 landed(hres.at[c, s], s_hres1.at[c, s])
+
+        @pl.when(is_end)
+        def _():
+            for s in range(N_SUB):
+                landed(hrec0.at[c, s], s_hsum.at[c, s])
 
         @pl.when(stage < n_stage - 1)
         def _():

time: 281 us -> 255 us (0.907)
  Pallas kernels: 269 us -> 244 us
    pallas_call x1, Pallas kernels: 269 us -> 244 us  [stage_fn(): call(hidden_in.reshape(N_CHUNK, rows, d_model), pos_wide, cos_t, sin_t, k...]
where the time goes in v2:
time: 255 us
  Pallas kernels  244 us (96%)
  local copies, waits for them, and re-layouts  8.37 us (3%)
    pallas_call x1, Pallas kernels, stage_fn(): call(hidden_in.reshape(N_CHUNK, rows, d_model), pos_wide, cos_t, sin_t, k...  244 us

profile of v2, /device:TPU:0, one launch (start us, length us, event | category | flops | bytes accessed | tf_op | source)
XLA Modules:
  0.0 255.0 jit_solution(11891635682978553342)
XLA Ops:
  0.6 0.7 convert_element_type.10
  1.3 1.3 broadcast_in_dim.5.gain_f
  2.6 1.4 broadcast_in_dim.4.pos
  4.1 0.5 fusion
  4.6 0.8 pad_maximum_fusion
  5.4 244.0 %shard_map.157 = (bf16[4,64,2560]{2,1,0:T(8,128)(2,1)}, bf16[4,64,256]{2,1,0:T(8,128)(2,1)}, bf16[4,64,256]{2,1,0:T(8,128)(2,1)}) custom-call(bf16[4,64,2560]{2,1,0:T(8,128)(2,1)} %bitcast.19, s32[256,128]{1,0:T(8,128)} %broadcast_in_dim.4.pos, f32[256,128]{1,0:T(8,128)} %get-tuple-element.12.cos_t, f32[256,128]{1,0:T(8,128)} %get-tuple-element.13.sin_t, ...), custom_call_target="tpu_custom_call" | custom-call | tf_op jit(solution)/shard_map/pallas_call | solution.py:545
  249.4 1.6 reshape.38
  251.0 1.6 reshape.39
  252.6 2.5 copy.18
  (1 shorter events, 0.0 us)

commit v3 on v2

--- a/solution.py
+++ b/solution.py
@@ -2,6 +2,7 @@
 
 import jax
 import jax.numpy as jnp
+import numpy as np
 from jax import lax
 from jax.experimental import pallas as pl
 from jax.experimental.pallas import tpu as pltpu
@@ -14,15 +15,9 @@
 MESH = pl.DeviceIdType.MESH
 
 N_CHUNK = 4
-N_SUB = 5
+N_A = 6
+N_B = 4
 GROUP = 16
-
-
-def rope_tables(positions, head_dim):
-    freq_idx = jnp.arange(0, head_dim, 2).astype(F32)
-    inv_freq = ROPE_THETA ** (-freq_idx / head_dim)
-    angles = positions.astype(F32)[:, None] * inv_freq[None, :]
-    return jnp.cos(angles), jnp.sin(angles)
 
 
 def norm_rows(rows, gain):
@@ -41,17 +36,16 @@
 
 def step_kernel(
     n_stage, n_tp,
-    hid, pos, cos_t, sin_t, k_hbm, v_hbm, gain_a, w_q, w_k, w_v, w_o, gain_m, w_g, w_u, w_d, gain_f,
+    hid, pos_row, inv_freq, k_hbm, v_hbm, gain_a, w_q, w_k, w_v, w_o, gain_m, w_g, w_u, w_d, gain_f,
     out, k_out, v_out,
-    wq, wk, wv, wg, wu, wd, kb, vb, hb, nb, qb, kn, vn, cb, ab, slots,
-    part, rec_e, rec_m, res_a, res_b, hrec0, hrec1, hrec_m, hres,
+    wq, wk, wv, wg, wu, wd, kb, vb, hb, nb, qb, kn, vn, ko, vo, mix, cb, ab, slots, pos, cos_t, sin_t,
+    part, rec_e, rec_m, res_a, res_b, hrec0, hrec1, hres,
     s_w, s_kv, s_rows, s_out, s_fwd,
-    r_h, s_h, r_out, s_part, s_sum, s_res, r_e, r_m, r_a, r_b,
+    r_h, s_h, r_out, s_part, s_sum, s_res, s_res2, r_e, r_m, r_a, r_b,
     s_hsum, s_hres0, s_hres1, r_h0, r_h1, r_hm,
 ):
     rows = hb.shape[1]
     sub = part.shape[3]
-    half = N_SUB * sub
     d_attn = cb.shape[1]
     kv_width = kn.shape[2]
     head_dim = kb.shape[2]
@@ -122,95 +116,113 @@
     same_head = lax.rem(col_id, kv_heads) == row_id // (GROUP * per_kv)
     slots[...] = jnp.where(jnp.logical_and(same_row, same_head), lax.rem(col_id, keys_per_row) // kv_heads, cache_len)
 
+    square = (128, 128)
+    on_diag = lax.broadcasted_iota(jnp.int32, square, 0) == lax.broadcasted_iota(jnp.int32, square, 1)
+    first_half = lax.broadcasted_iota(jnp.int32, square, 1) < head_dim // 2
+    for b in range(pos_row.shape[0]):
+        wide = jnp.where(on_diag, jnp.broadcast_to(pos_row[pl.ds(b, 1), :], square), 0).astype(F32)
+        column = jnp.broadcast_to(jnp.sum(wide, axis=1, keepdims=True), square)
+        at = pl.ds(b * 128, 128)
+        pos[at, :] = column.astype(jnp.int32)
+        angles = column * inv_freq[...]
+        cos_t[at, :] = jnp.cos(angles)
+        sines = jnp.sin(angles)
+        sin_t[at, :] = jnp.where(first_half, -sines, sines)
+
     def send_part(k, b_half):
         kc = lax.rem(k, N_CHUNK)
-        base = N_SUB if b_half else 0
         if b_half:
             @pl.when(is_end)
             def _():
-                for s in range(N_SUB):
-                    remote(part.at[kc, base + s], hrec_m.at[k, s], s_part.at[kc, base + s], r_hm.at[k, s], helped, line).start()
+                for s in range(N_B):
+                    remote(part.at[kc, N_A + s], rec_m.at[k, s], s_part.at[kc, N_A + s], r_hm.at[k, s], helped, line).start()
 
             @pl.when(is_mid)
             def _():
-                for s in range(N_SUB):
-                    remote(part.at[kc, base + s], hrec1.at[kc, s], s_part.at[kc, base + s], r_h1.at[kc, s], helped, line).start()
+                for s in range(N_B):
+                    remote(part.at[kc, N_A + s], hrec1.at[kc, s], s_part.at[kc, N_A + s], r_h1.at[kc, s], helped, line).start()
         else:
             @pl.when(is_end)
             def _():
-                for s in range(N_SUB):
+                for s in range(N_A):
                     remote(part.at[kc, s], rec_e.at[kc, s], s_part.at[kc, s], r_e.at[kc, s], stage, mid_of).start()
 
     def wait_part_sends(k):
         kc = lax.rem(k, N_CHUNK)
-        for s in range(N_SUB):
-            landed(part.at[kc, N_SUB + s], s_part.at[kc, N_SUB + s])
+        for s in range(N_B):
+            landed(part.at[kc, N_A + s], s_part.at[kc, N_A + s])
 
         @pl.when(is_end)
         def _():
-            for s in range(N_SUB):
+            for s in range(N_A):
                 landed(part.at[kc, s], s_part.at[kc, s])
 
         @pl.when(is_mid)
         def _():
-            for s in range(N_SUB):
+            for s in range(N_A):
                 landed(part.at[kc, s], s_sum.at[kc, s])
 
     def sum_first(k):
         kc = lax.rem(k, N_CHUNK)
-        for s in range(N_SUB):
+        for s in range(N_A):
             landed(rec_e.at[kc, s], r_e.at[kc, s])
             part[kc, s] = part[kc, s] + rec_e[kc, s]
             remote(part.at[kc, s], rec_m.at[k, s], s_sum.at[kc, s], r_m.at[k, s], stage, other_mid).start()
 
     def sum_second(k):
         kc = lax.rem(k, N_CHUNK)
+        to_stage = jnp.where(k < N_CHUNK, stage, jnp.minimum(stage + 1, n_stage - 1))
 
         @pl.when(k >= N_CHUNK)
         def _():
-            for s in range(N_SUB):
+            for s in range(N_A):
                 landed(res_a.at[kc, s], s_res.at[kc, s])
 
-        for s in range(N_SUB):
+        for s in range(N_A):
             landed(rec_m.at[k, s], r_m.at[k, s])
-            res_a[kc, s] = (part[kc, s] + rec_m[k, s]).astype(BF16)
-            remote(res_a.at[kc, s], res_a.at[kc, s], s_res.at[kc, s], r_a.at[kc, s], stage, end_of).start()
+            res_a[k, s] = (part[kc, s] + rec_m[k, s]).astype(BF16)
+            remote(res_a.at[k, s], res_a.at[k, s], s_res.at[kc, s], r_a.at[k, s], to_stage, end_of).start()
+
+            @pl.when(jnp.logical_and(k >= N_CHUNK, stage < n_stage - 1))
+            def _():
+                remote(res_a.at[k, s], res_a.at[k, s], s_res2.at[kc, s], r_a.at[k, s], to_stage, line).start()
 
     def help_first(k):
         kc = lax.rem(k, N_CHUNK)
-        for s in range(N_SUB):
+        for s in range(N_B):
             landed(hrec0.at[kc, s], r_h0.at[kc, s])
             landed(hrec1.at[kc, s], r_h1.at[kc, s])
             hrec1[kc, s] = hrec1[kc, s] + hrec0[kc, s]
-            remote(hrec1.at[kc, s], hrec_m.at[k, s], s_hsum.at[kc, s], r_hm.at[k, s], stage, other_mid).start()
+            remote(hrec1.at[kc, s], rec_m.at[k, s], s_hsum.at[kc, s], r_hm.at[k, s], stage, other_mid).start()
 
     def help_second(k):
         kc = lax.rem(k, N_CHUNK)
+        to_stage = jnp.where(k < N_CHUNK, helped, jnp.minimum(helped + 1, n_stage - 1))
 
         @pl.when(k >= N_CHUNK)
         def _():
-            for s in range(N_SUB):
+            for s in range(N_B):
                 landed(hres.at[kc, s], s_hres0.at[kc, s])
                 landed(hres.at[kc, s], s_hres1.at[kc, s])
 
-        for s in range(N_SUB):
-            landed(hrec_m.at[k, s], r_hm.at[k, s])
+        for s in range(N_B):
+            landed(rec_m.at[k, s], r_hm.at[k, s])
             landed(hrec1.at[kc, s], s_hsum.at[kc, s])
-            hres[kc, s] = (hrec1[kc, s] + hrec_m[k, s]).astype(BF16)
-            remote(hres.at[kc, s], res_b.at[kc, s], s_hres0.at[kc, s], r_b.at[kc, s], helped, end_of).start()
-            remote(hres.at[kc, s], res_b.at[kc, s], s_hres1.at[kc, s], r_b.at[kc, s], helped, line).start()
+            hres[kc, s] = (hrec1[kc, s] + rec_m[k, s]).astype(BF16)
+            remote(hres.at[kc, s], res_b.at[k, s], s_hres0.at[kc, s], r_b.at[k, s], to_stage, end_of).start()
+            remote(hres.at[kc, s], res_b.at[k, s], s_hres1.at[kc, s], r_b.at[k, s], to_stage, line).start()
 
     def help_forward(k):
         kc = lax.rem(k, N_CHUNK)
 
         @pl.when(k >= N_CHUNK)
         def _():
-            for s in range(N_SUB):
+            for s in range(N_B):
                 landed(hrec0.at[kc, s], s_hsum.at[kc, s])
 
-        for s in range(N_SUB):
-            landed(hrec_m.at[k, s], r_hm.at[k, s])
-            remote(hrec_m.at[k, s], hrec0.at[kc, s], s_hsum.at[kc, s], r_h0.at[kc, s], stage, mid_of).start()
+        for s in range(N_B):
+            landed(rec_m.at[k, s], r_hm.at[k, s])
+            remote(rec_m.at[k, s], hrec0.at[kc, s], s_hsum.at[kc, s], r_h0.at[kc, s], stage, mid_of).start()
 
     def help_stage():
         @pl.when(is_end)
@@ -242,32 +254,36 @@
             def _():
                 sum_second(k - 2)
 
-    def add_sum(c):
-        @pl.when(is_end)
-        def _():
-            for s in range(N_SUB):
-                landed(res_a.at[c, s], r_a.at[c, s])
-
-        for s in range(N_SUB):
+    def add_sum(c, k, remote_a):
+        @pl.when(remote_a)
+        def _():
+            for s in range(N_A):
+                landed(res_a.at[k, s], r_a.at[k, s])
+
+        for s in range(N_A):
             at = pl.ds(s * sub, sub)
-            hb[c, :, at] = (hb[c, :, at].astype(F32) + res_a[c, s].astype(F32)).astype(BF16)
-        for s in range(N_SUB):
-            at = pl.ds(half + s * sub, sub)
-            landed(res_b.at[c, s], r_b.at[c, s])
-            hb[c, :, at] = (hb[c, :, at].astype(F32) + res_b[c, s].astype(F32)).astype(BF16)
+            hb[c, :, at] = (hb[c, :, at].astype(F32) + res_a[k, s].astype(F32)).astype(BF16)
+        for s in range(N_B):
+            at = pl.ds((N_A + s) * sub, sub)
+            landed(res_b.at[k, s], r_b.at[k, s])
+            hb[c, :, at] = (hb[c, :, at].astype(F32) + res_b[k, s].astype(F32)).astype(BF16)
 
     def partials(k, act, weight, depth):
         kc = lax.rem(k, N_CHUNK)
         for b_half in (True, False):
-            base = N_SUB if b_half else 0
-            got = dot(act, weight[pl.ds(0, depth), pl.ds(half if b_half else 0, half)])
-            for s in range(N_SUB):
+            base, count = (N_A, N_B) if b_half else (0, N_A)
+            got = dot(act, weight[pl.ds(0, depth), pl.ds(base * sub, count * sub)])
+            for s in range(count):
                 part[kc, base + s] = got[:, s * sub:(s + 1) * sub]
             send_part(k, b_half)
 
     def attention(c):
         slot = lax.rem(c, 2)
         landed(hb.at[c], r_h.at[c])
+
+        @pl.when(stage > 0)
+        def _():
+            add_sum(c, N_CHUNK + c, stage > 0)
 
         @pl.when(c == 0)
         def _():
@@ -288,10 +304,15 @@
         got_v = dot(nb[...], wv[...])
         for g in range(kv_heads):
             at = pl.ds(g * head_dim, head_dim)
-            kn[c, :, at] = rope(got_k[:, g * head_dim:(g + 1) * head_dim])
+            rotated = rope(got_k[:, g * head_dim:(g + 1) * head_dim])
+            kn[c, :, at] = rotated
+            mix[0, pl.ds(g, rows, stride=kv_heads), :] = rotated.astype(F32)
+            mix[1, pl.ds(g, rows, stride=kv_heads), :] = got_v[:, g * head_dim:(g + 1) * head_dim]
         vn[c] = got_v.astype(BF16)
-        pltpu.make_async_copy(kn.at[c], k_out.at[c], s_rows.at[0, c]).start()
-        pltpu.make_async_copy(vn.at[c], v_out.at[c], s_rows.at[1, c]).start()
+        ko[c] = mix[0].astype(BF16)
+        vo[c] = mix[1].astype(BF16)
+        pltpu.make_async_copy(ko.at[c], k_out.at[c], s_rows.at[0, c]).start()
+        pltpu.make_async_copy(vo.at[c], v_out.at[c], s_rows.at[1, c]).start()
         got_q = dot(nb[...], wq[...])
         for h in range(n_head):
             qb[:, pl.ds(h * head_dim, head_dim)] = rope(got_q[:, h * head_dim:(h + 1) * head_dim])
@@ -370,7 +391,7 @@
 
     def mlp_part(k):
         c = k - N_CHUNK
-        add_sum(c)
+        add_sum(c, c, is_end)
         nb[...] = norm_rows(hb[c], gain_m[...])
 
         @pl.when(c == 0)
@@ -391,16 +412,15 @@
         wait_part_sends(k - N_CHUNK)
         partials(k, ab[...], wd, wd.shape[0])
 
+        @pl.when(stage < n_stage - 1)
+        def _():
+            remote(hb.at[c], hb.at[c], s_h.at[c], r_h.at[c], stage + 1, line).start()
+
     def finish(c):
-        add_sum(c)
-
-        @pl.when(stage < n_stage - 1)
-        def _():
-            remote(hb.at[c], hb.at[c], s_h.at[c], r_h.at[c], stage + 1, line).start()
-
         @pl.when(stage == n_stage - 1)
         def _():
-            hb[c] = norm_rows(hb[c], gain_f[...])
+            add_sum(c, N_CHUNK + c, is_end)
+            hb[c] = norm_rows(hb[c], gain_f[...].reshape(1, hb.shape[2]))
             remote(hb.at[c], out.at[c], s_fwd.at[0, c], r_out.at[c], stage - 2, line).start()
             remote(hb.at[c], out.at[c], s_fwd.at[1, c], r_out.at[c], stage - 1, line).start()
             pltpu.make_async_copy(hb.at[c], out.at[c], s_out.at[c]).start()
@@ -434,19 +454,26 @@
     @pl.loop(0, N_CHUNK)
     def _(c):
         wait_part_sends(c)
-        for i, (ref, dst) in enumerate(((kn, k_out), (vn, v_out))):
+        for i, (ref, dst) in enumerate(((ko, k_out), (vo, v_out))):
             landed(ref.at[c], s_rows.at[i, c])
 
         @pl.when(is_mid)
         def _():
-            for s in range(N_SUB):
+            for s in range(N_A):
                 landed(res_a.at[c, s], s_res.at[c, s])
+
+            @pl.when(stage < n_stage - 1)
+            def _():
+                for s in range(N_A):
+                    landed(res_a.at[c, s], s_res2.at[c, s])
+
+            for s in range(N_B):
                 landed(hres.at[c, s], s_hres0.at[c, s])
                 landed(hres.at[c, s], s_hres1.at[c, s])
 
         @pl.when(is_end)
         def _():
-            for s in range(N_SUB):
+            for s in range(N_B):
                 landed(hrec0.at[c, s], s_hsum.at[c, s])
 
         @pl.when(stage < n_stage - 1)
@@ -486,27 +513,26 @@
         d_attn = w_q.shape[2]
         kv_width = kv_local * head_dim
         d_ff = w_gate.shape[2]
-        half = d_model // 2
-        sub = half // N_SUB
+        sub = d_model // (N_A + N_B)
         n_head = d_attn // head_dim
         keys = rows * cache_len * kv_local
         score_keys = 4 * cache_len * kv_local
-        cos_h, sin_h = rope_tables(positions, head_dim)
-        cos_t = jnp.concatenate([cos_h, cos_h], axis=-1)
-        sin_t = jnp.concatenate([-sin_h, sin_h], axis=-1)
-        pos_wide = jnp.broadcast_to(positions[:, None], (batch, 128))
+        inverse = ROPE_THETA ** (-np.arange(0, head_dim, 2).astype(np.float32) / head_dim)
+        inv_freq = jnp.asarray(np.concatenate([inverse, inverse])[None].astype(np.float32))
         anywhere = pl.BlockSpec(memory_space=pl.ANY)
         vmem = pl.BlockSpec(memory_space=pltpu.VMEM)
         dma = pltpu.SemaphoreType.DMA
-        blocks = (N_CHUNK, N_SUB)
+        a_blocks = (N_CHUNK, N_A)
+        b_blocks = (N_CHUNK, N_B)
+        tile = (rows, sub)
         call = pl.pallas_call(
             functools.partial(step_kernel, n_stage, n_tp),
             out_shape=[
                 jax.ShapeDtypeStruct((N_CHUNK, rows, d_model), BF16),
-                jax.ShapeDtypeStruct((N_CHUNK, rows, kv_width), BF16),
-                jax.ShapeDtypeStruct((N_CHUNK, rows, kv_width), BF16),
+                jax.ShapeDtypeStruct((N_CHUNK, rows * kv_local, head_dim), BF16),
+                jax.ShapeDtypeStruct((N_CHUNK, rows * kv_local, head_dim), BF16),
             ],
-            in_specs=[anywhere, vmem, vmem, vmem, anywhere, anywhere, vmem] + [anywhere] * 4 + [vmem] + [anywhere] * 3 + [vmem],
+            in_specs=[anywhere, vmem, vmem, anywhere, anywhere, vmem] + [anywhere] * 4 + [vmem] + [anywhere] * 3 + [vmem],
             out_specs=[anywhere] * 3,
             scratch_shapes=[
                 pltpu.VMEM((d_model, d_attn), BF16),
@@ -522,30 +548,35 @@
                 pltpu.VMEM((rows, d_attn), BF16),
                 pltpu.VMEM((N_CHUNK, rows, kv_width), BF16),
                 pltpu.VMEM((N_CHUNK, rows, kv_width), BF16),
+                pltpu.VMEM((N_CHUNK, rows * kv_local, head_dim), BF16),
+                pltpu.VMEM((N_CHUNK, rows * kv_local, head_dim), BF16),
+                pltpu.VMEM((2, rows * kv_local, head_dim), F32),
                 pltpu.VMEM((rows, d_attn), BF16),
                 pltpu.VMEM((rows, d_ff), BF16),
                 pltpu.VMEM((GROUP * n_head, score_keys), jnp.int32),
-                pltpu.VMEM((N_CHUNK, 2 * N_SUB, rows, sub), F32),
-                pltpu.VMEM(blocks + (rows, sub), F32),
-                pltpu.VMEM((2 * N_CHUNK, N_SUB, rows, sub), F32),
-                pltpu.VMEM(blocks + (rows, sub), BF16),
-                pltpu.VMEM(blocks + (rows, sub), BF16),
-                pltpu.VMEM(blocks + (rows, sub), F32),
-                pltpu.VMEM(blocks + (rows, sub), F32),
-                pltpu.VMEM((2 * N_CHUNK, N_SUB, rows, sub), F32),
-                pltpu.VMEM(blocks + (rows, sub), BF16),
+                pltpu.VMEM((batch, 128), jnp.int32),
+                pltpu.VMEM((batch, head_dim), F32),
+                pltpu.VMEM((batch, head_dim), F32),
+                pltpu.VMEM((N_CHUNK, N_A + N_B) + tile, F32),
+                pltpu.VMEM(a_blocks + tile, F32),
+                pltpu.VMEM((2 * N_CHUNK, max(N_A, N_B)) + tile, F32),
+                pltpu.VMEM((2 * N_CHUNK, N_A) + tile, BF16),
+                pltpu.VMEM((2 * N_CHUNK, N_B) + tile, BF16),
+                pltpu.VMEM(b_blocks + tile, F32),
+                pltpu.VMEM(b_blocks + tile, F32),
+                pltpu.VMEM(b_blocks + tile, BF16),
                 dma((8,)), dma((2, 2)), dma((2, N_CHUNK)), dma((N_CHUNK,)), dma((2, N_CHUNK)),
                 dma((N_CHUNK,)), dma((N_CHUNK,)), dma((N_CHUNK,)),
-                dma((N_CHUNK, 2 * N_SUB)), dma(blocks), dma(blocks),
-                dma(blocks), dma((2 * N_CHUNK, N_SUB)), dma(blocks), dma(blocks),
-                dma(blocks), dma(blocks), dma(blocks), dma(blocks), dma(blocks), dma((2 * N_CHUNK, N_SUB)),
+                dma((N_CHUNK, N_A + N_B)), dma(a_blocks), dma(a_blocks), dma(a_blocks),
+                dma(a_blocks), dma((2 * N_CHUNK, N_A)), dma((2 * N_CHUNK, N_A)), dma((2 * N_CHUNK, N_B)),
+                dma(b_blocks), dma(b_blocks), dma(b_blocks), dma(b_blocks), dma(b_blocks), dma((2 * N_CHUNK, N_B)),
             ],
             compiler_params=pltpu.CompilerParams(collective_id=0, has_side_effects=True, vmem_limit_bytes=67043328),
         )
         out, k_rows, v_rows = call(
-            hidden_in.reshape(N_CHUNK, rows, d_model), pos_wide, cos_t, sin_t,
+            hidden_in.reshape(N_CHUNK, rows, d_model), positions.reshape(-1, 128), inv_freq,
             k_cache.reshape(N_CHUNK, keys, head_dim), v_cache.reshape(N_CHUNK, keys, head_dim),
-            attn_gain, w_q[0], w_k[0], w_v[0], w_o[0], mlp_gain, w_gate[0], w_up[0], w_down[0], final_gain[None])
+            attn_gain, w_q[0], w_k[0], w_v[0], w_o[0], mlp_gain, w_gate[0], w_up[0], w_down[0], final_gain)
         shape = (1, batch, kv_local, head_dim)
         return out.reshape(batch, d_model), k_rows.reshape(shape), v_rows.reshape(shape)
 

time: 255 us -> 242 us (0.949)
  Pallas kernels: 244 us -> 236 us
  local copies, waits for them, and re-layouts: 8.37 us -> 5.76 us
    pallas_call x1, Pallas kernels: 244 us -> 236 us  [stage_fn(): call(hidden_in.reshape(N_CHUNK, rows, d_model), positions.reshape(-1, 128...]
    unnamed x1 -> x3, local copies, waits for them, and re-layouts: 2.46 us -> 5.76 us
    reshape x2 -> x0, local copies, waits for them, and re-layouts: 3.19 us -> none  [the longest x1 1.6 us: stage_fn(): k_rows.reshape(shape)]
    broadcast_in_dim x2 -> x0, local copies, waits for them, and re-layouts: 2.73 us -> none  [the longest x1 1.43 us: stage_fn(): pos_wide = jnp.broadcast_to(positions[:, None], (batch, 128))]
where the time goes in v3:
time: 242 us
  Pallas kernels  236 us (98%)
  local copies, waits for them, and re-layouts  5.76 us (2%)
    pallas_call x1, Pallas kernels, stage_fn(): call(hidden_in.reshape(N_CHUNK, rows, d_model), positions.reshape(-1, 128...  236 us
    unnamed x3, local copies, waits for them, and re-layouts  5.76 us

profile of v3, /device:TPU:0, one launch (start us, length us, event | category | flops | bytes accessed | tf_op | source)
XLA Modules:
  0.0 242.1 jit_solution(9694557742253459922)
XLA Ops:
  0.6 235.7 %shard_map.166 = (bf16[4,64,2560]{2,1,0:T(8,128)(2,1)}, bf16[4,128,128]{2,1,0:T(8,128)(2,1)}, bf16[4,128,128]{2,1,0:T(8,128)(2,1)}) custom-call(bf16[4,64,2560]{2,1,0:T(8,128)(2,1)} %bitcast.22, s32[2,128]{1,0:T(2,128)} %bitcast.27, f32[1,128]{1,0:T(1,128)} %constant.2.clone.inv_freq, bf16[4,4096,128]{2,1,0:T(8,128)(2,1)} %bitcast.19, ...), custom_call_target="tpu_custom_call" | custom-call | tf_op jit(solution)/shard_map/pallas_call | solution.py:576
  236.3 2.5 %copy.21 = bf16[256,2560]{1,0:T(8,128)(2,1)} copy(bf16[256,2560]{1,0:T(8,128)(2,1)} %bitcast.21) | data formatting | bytes 2621440
  238.8 1.6 copy.22
  240.4 1.6 copy.23

commit v4 on v3

--- a/solution.py
+++ b/solution.py
@@ -15,8 +15,8 @@
 MESH = pl.DeviceIdType.MESH
 
 N_CHUNK = 4
-N_A = 6
-N_B = 4
+N_A = 5
+N_B = 5
 GROUP = 16
 
 
@@ -41,8 +41,8 @@
     wq, wk, wv, wg, wu, wd, kb, vb, hb, nb, qb, kn, vn, ko, vo, mix, cb, ab, slots, pos, cos_t, sin_t,
     part, rec_e, rec_m, res_a, res_b, hrec0, hrec1, hres,
     s_w, s_kv, s_rows, s_out, s_fwd,
-    r_h, s_h, r_out, s_part, s_sum, s_res, s_res2, r_e, r_m, r_a, r_b,
-    s_hsum, s_hres0, s_hres1, r_h0, r_h1, r_hm,
+    r_h, s_h, r_out, s_part, s_sum, s_res, s_res2, s_res3, r_e, r_m, r_a, r_b,
+    s_hsum, s_hres0, s_hres1, s_hres2, r_h0, r_h1, r_hm,
 ):
     rows = hb.shape[1]
     sub = part.shape[3]
@@ -62,6 +62,9 @@
     mid_of = jnp.where(line < n_tp // 2, 1, n_tp - 2)
     end_of = jnp.where(line < n_tp // 2, 0, n_tp - 1)
     other_mid = n_tp - 1 - line
+    last = n_stage - 1
+    mirror = last - 2
+    after = jnp.where(stage < last, stage + 1, mirror)
 
     def remote(src, dst, send, recv, to_stage, to_line):
         return pltpu.make_async_remote_copy(
@@ -183,9 +186,13 @@
             res_a[k, s] = (part[kc, s] + rec_m[k, s]).astype(BF16)
             remote(res_a.at[k, s], res_a.at[k, s], s_res.at[kc, s], r_a.at[k, s], to_stage, end_of).start()
 
-            @pl.when(jnp.logical_and(k >= N_CHUNK, stage < n_stage - 1))
-            def _():
-                remote(res_a.at[k, s], res_a.at[k, s], s_res2.at[kc, s], r_a.at[k, s], to_stage, line).start()
+            @pl.when(k >= N_CHUNK)
+            def _():
+                remote(res_a.at[k, s], res_a.at[k, s], s_res2.at[kc, s], r_a.at[k, s], after, line).start()
+
+            @pl.when(jnp.logical_and(k >= N_CHUNK, stage == last))
+            def _():
+                remote(res_a.at[k, s], res_a.at[k, s], s_res3.at[kc, s], r_a.at[k, s], after, end_of).start()
 
     def help_first(k):
         kc = lax.rem(k, N_CHUNK)
@@ -212,6 +219,11 @@
             remote(hres.at[kc, s], res_b.at[k, s], s_hres0.at[kc, s], r_b.at[k, s], to_stage, end_of).start()
             remote(hres.at[kc, s], res_b.at[k, s], s_hres1.at[kc, s], r_b.at[k, s], to_stage, line).start()
 
+            @pl.when(jnp.logical_and(k >= N_CHUNK, stage == mirror))
+            def _():
+                res_b[k, s] = hres[kc, s]
+                remote(hres.at[kc, s], res_b.at[k, s], s_hres2.at[kc, s], r_b.at[k, s], stage, end_of).start()
+
     def help_forward(k):
         kc = lax.rem(k, N_CHUNK)
 
@@ -224,25 +236,30 @@
             landed(rec_m.at[k, s], r_hm.at[k, s])
             remote(rec_m.at[k, s], hrec0.at[kc, s], s_hsum.at[kc, s], r_h0.at[kc, s], stage, mid_of).start()
 
-    def help_stage():
+    def help_stage(finish_early):
         @pl.when(is_end)
         def _():
             @pl.loop(0, 2 * N_CHUNK)
             def _(k):
                 help_forward(k)
+                finish_early(k)
 
         @pl.when(is_mid)
         def _():
-            @pl.loop(0, 2 * N_CHUNK + 1)
+            @pl.loop(0, 2 * N_CHUNK)
             def _(k):
-                @pl.when(k < 2 * N_CHUNK)
-                def _():
-                    help_first(k)
-
-                @pl.when(k >= 1)
+                help_first(k)
+
+                @pl.when(k == N_CHUNK + 1)
                 def _():
                     help_second(k - 1)
 
+                @pl.when(k != N_CHUNK)
+                def _():
+                    help_second(k)
+
+                finish_early(k)
+
     def relay(k):
         @pl.when(is_mid)
         def _():
@@ -254,7 +271,7 @@
             def _():
                 sum_second(k - 2)
 
-    def add_sum(c, k, remote_a):
+    def add_sum(c, k, remote_a, remote_b=None):
         @pl.when(remote_a)
         def _():
             for s in range(N_A):
@@ -265,7 +282,12 @@
             hb[c, :, at] = (hb[c, :, at].astype(F32) + res_a[k, s].astype(F32)).astype(BF16)
         for s in range(N_B):
             at = pl.ds((N_A + s) * sub, sub)
-            landed(res_b.at[k, s], r_b.at[k, s])
+            if remote_b is None:
+                landed(res_b.at[k, s], r_b.at[k, s])
+            else:
+                @pl.when(remote_b)
+                def _():
+                    landed(res_b.at[k, s], r_b.at[k, s])
             hb[c, :, at] = (hb[c, :, at].astype(F32) + res_b[k, s].astype(F32)).astype(BF16)
 
     def partials(k, act, weight, depth):
@@ -412,18 +434,23 @@
         wait_part_sends(k - N_CHUNK)
         partials(k, ab[...], wd, wd.shape[0])
 
-        @pl.when(stage < n_stage - 1)
-        def _():
-            remote(hb.at[c], hb.at[c], s_h.at[c], r_h.at[c], stage + 1, line).start()
-
-    def finish(c):
-        @pl.when(stage == n_stage - 1)
-        def _():
+        remote(hb.at[c], hb.at[c], s_h.at[c], r_h.at[c], after, line).start()
+
+    def finish(c, at_last):
+        if at_last:
+            landed(hb.at[c], s_h.at[c])
             add_sum(c, N_CHUNK + c, is_end)
-            hb[c] = norm_rows(hb[c], gain_f[...].reshape(1, hb.shape[2]))
-            remote(hb.at[c], out.at[c], s_fwd.at[0, c], r_out.at[c], stage - 2, line).start()
-            remote(hb.at[c], out.at[c], s_fwd.at[1, c], r_out.at[c], stage - 1, line).start()
-            pltpu.make_async_copy(hb.at[c], out.at[c], s_out.at[c]).start()
+        else:
+            landed(hb.at[c], r_h.at[c])
+            add_sum(c, N_CHUNK + c, stage == mirror, is_end)
+        hb[c] = norm_rows(hb[c], gain_f[...].reshape(1, hb.shape[2]))
+        remote(hb.at[c], out.at[c], s_fwd.at[c], r_out.at[c], stage - 1, line).start()
+        pltpu.make_async_copy(hb.at[c], out.at[c], s_out.at[c]).start()
+
+    def finish_mirror(k):
+        @pl.when(jnp.logical_and(stage == mirror, k > N_CHUNK))
+        def _():
+            finish(k - N_CHUNK - 1, False)
 
     def compute_stage():
         @pl.loop(0, N_CHUNK)
@@ -438,63 +465,106 @@
 
         @pl.loop(2 * N_CHUNK, 3 * N_CHUNK)
         def _(k):
-            finish(k - 2 * N_CHUNK)
+            @pl.when(stage == last)
+            def _():
+                finish(k - 2 * N_CHUNK, True)
+
             relay(k)
+
+    def drain_compute():
+        @pl.loop(0, N_CHUNK)
+        def _(c):
+            wait_part_sends(c)
+            for i, (ref, dst) in enumerate(((ko, k_out), (vo, v_out))):
+                landed(ref.at[c], s_rows.at[i, c])
+
+            @pl.when(stage < last)
+            def _():
+                landed(hb.at[c], s_h.at[c])
+
+            @pl.when(is_mid)
+            def _():
+                for s in range(N_A):
+                    landed(res_a.at[c, s], s_res.at[c, s])
+                    landed(res_a.at[c, s], s_res2.at[c, s])
+
+                @pl.when(stage == last)
+                def _():
+                    for s in range(N_A):
+                        landed(res_a.at[c, s], s_res3.at[c, s])
 
     @pl.when(side == 1)
     def _():
-        help_stage()
+        help_stage(lambda k: None)
 
     compute_stage()
+    drain_compute()
 
     @pl.when(side == 0)
     def _():
-        help_stage()
+        help_stage(finish_mirror)
+
+        @pl.when(stage == mirror)
+        def _():
+            finish(N_CHUNK - 1, False)
 
     @pl.loop(0, N_CHUNK)
     def _(c):
-        wait_part_sends(c)
-        for i, (ref, dst) in enumerate(((ko, k_out), (vo, v_out))):
-            landed(ref.at[c], s_rows.at[i, c])
-
         @pl.when(is_mid)
         def _():
-            for s in range(N_A):
-                landed(res_a.at[c, s], s_res.at[c, s])
-
-            @pl.when(stage < n_stage - 1)
-            def _():
-                for s in range(N_A):
-                    landed(res_a.at[c, s], s_res2.at[c, s])
-
             for s in range(N_B):
                 landed(hres.at[c, s], s_hres0.at[c, s])
                 landed(hres.at[c, s], s_hres1.at[c, s])
 
+            @pl.when(stage == mirror)
+            def _():
+                for s in range(N_B):
+                    landed(hres.at[c, s], s_hres2.at[c, s])
+
         @pl.when(is_end)
         def _():
             for s in range(N_B):
                 landed(hrec0.at[c, s], s_hsum.at[c, s])
 
-        @pl.when(stage < n_stage - 1)
-        def _():
-            landed(hb.at[c], s_h.at[c])
+        spreads = jnp.logical_or(stage == last, stage == mirror)
+
+        @pl.when(spreads)
+        def _():
+            landed(hb.at[c], s_out.at[c])
+            landed(hb.at[c], s_fwd.at[c])
+
+        @pl.when(jnp.logical_not(spreads))
+        def _():
             landed(out.at[c], r_out.at[c])
 
-        @pl.when(stage == n_stage - 3)
-        def _():
-            remote(out.at[c], out.at[c], s_fwd.at[0, c], r_out.at[c], stage - 1, line).start()
-
-        @pl.when(stage == n_stage - 1)
-        def _():
-            landed(hb.at[c], s_out.at[c])
-            landed(hb.at[c], s_fwd.at[0, c])
-            landed(hb.at[c], s_fwd.at[1, c])
-
-    @pl.when(stage == n_stage - 3)
-    def _():
-        for c in range(N_CHUNK):
-            landed(out.at[c], s_fwd.at[0, c])
+
+def copy_kernel(*refs):
+    count = len(refs) // 4
+    sources, results, staged, sems = (refs[i * count:(i + 1) * count] for i in range(4))
+    n = N_CHUNK
+    into = [[pltpu.make_async_copy(a.at[c], v.at[c], m.at[0, c]) for c in range(n)] for a, v, m in zip(sources, staged, sems)]
+    back = [[pltpu.make_async_copy(v.at[c], o.at[c], m.at[1, c]) for c in range(n)] for o, v, m in zip(results, staged, sems)]
+    for c in range(n):
+        for one in into:
+            one[c].start()
+    for c in range(n):
+        for one, two in zip(into, back):
+            one[c].wait()
+            two[c].start()
+    for c in range(n):
+        for two in back:
+            two[c].wait()
+
+
+def copied(arrays):
+    anywhere = pl.BlockSpec(memory_space=pl.ANY)
+    return pl.pallas_call(
+        copy_kernel,
+        out_shape=[jax.ShapeDtypeStruct(a.shape, a.dtype) for a in arrays],
+        in_specs=[anywhere] * len(arrays),
+        out_specs=[anywhere] * len(arrays),
+        scratch_shapes=[pltpu.VMEM(a.shape, a.dtype) for a in arrays] + [pltpu.SemaphoreType.DMA((2, N_CHUNK)) for _ in arrays],
+    )(*arrays)
 
 
 def solution(mesh):
@@ -565,18 +635,18 @@
                 pltpu.VMEM(b_blocks + tile, F32),
                 pltpu.VMEM(b_blocks + tile, F32),
                 pltpu.VMEM(b_blocks + tile, BF16),
-                dma((8,)), dma((2, 2)), dma((2, N_CHUNK)), dma((N_CHUNK,)), dma((2, N_CHUNK)),
+                dma((8,)), dma((2, 2)), dma((2, N_CHUNK)), dma((N_CHUNK,)), dma((N_CHUNK,)),
                 dma((N_CHUNK,)), dma((N_CHUNK,)), dma((N_CHUNK,)),
-                dma((N_CHUNK, N_A + N_B)), dma(a_blocks), dma(a_blocks), dma(a_blocks),
+                dma((N_CHUNK, N_A + N_B)), dma(a_blocks), dma(a_blocks), dma(a_blocks), dma(a_blocks),
                 dma(a_blocks), dma((2 * N_CHUNK, N_A)), dma((2 * N_CHUNK, N_A)), dma((2 * N_CHUNK, N_B)),
-                dma(b_blocks), dma(b_blocks), dma(b_blocks), dma(b_blocks), dma(b_blocks), dma((2 * N_CHUNK, N_B)),
+                dma(b_blocks), dma(b_blocks), dma(b_blocks), dma(b_blocks), dma(b_blocks), dma(b_blocks), dma((2 * N_CHUNK, N_B)),
             ],
             compiler_params=pltpu.CompilerParams(collective_id=0, has_side_effects=True, vmem_limit_bytes=67043328),
         )
-        out, k_rows, v_rows = call(
+        out, k_rows, v_rows = copied(call(
             hidden_in.reshape(N_CHUNK, rows, d_model), positions.reshape(-1, 128), inv_freq,
             k_cache.reshape(N_CHUNK, keys, head_dim), v_cache.reshape(N_CHUNK, keys, head_dim),
-            attn_gain, w_q[0], w_k[0], w_v[0], w_o[0], mlp_gain, w_gate[0], w_up[0], w_down[0], final_gain)
+            attn_gain, w_q[0], w_k[0], w_v[0], w_o[0], mlp_gain, w_gate[0], w_up[0], w_down[0], final_gain))
         shape = (1, batch, kv_local, head_dim)
         return out.reshape(batch, d_model), k_rows.reshape(shape), v_rows.reshape(shape)
 

time: 242 us -> 240 us (level)
  local copies, waits for them, and re-layouts: 5.76 us -> 0 us
  Pallas kernels: 236 us -> 239 us
    unnamed x3 -> x0, local copies, waits for them, and re-layouts: 5.76 us -> none
where the time goes in v4:
time: 240 us
  Pallas kernels  239 us (100%)
    pallas_call x1, Pallas kernels, stage_fn(): call(hidden_in.reshape(N_CHUNK, rows, d_model), positions.reshape(-1, 128...  237 us

profile of v4, /device:TPU:0, one launch (start us, length us, event | category | flops | bytes accessed | tf_op | source)
XLA Modules:
  0.0 239.6 jit_solution(6868159682313875109)
XLA Ops:
  0.6 236.7 %shard_map.166 = (bf16[4,64,2560]{2,1,0:T(8,128)(2,1)}, bf16[4,128,128]{2,1,0:T(8,128)(2,1)}, bf16[4,128,128]{2,1,0:T(8,128)(2,1)}) custom-call(bf16[4,64,2560]{2,1,0:T(8,128)(2,1)} %bitcast.21, s32[2,128]{1,0:T(2,128)} %bitcast.24, f32[1,128]{1,0:T(1,128)} %constant.2.clone.inv_freq, bf16[4,4096,128]{2,1,0:T(8,128)(2,1)} %bitcast.19, ...), custom_call_target="tpu_custom_call" | custom-call | tf_op jit(solution)/shard_map/pallas_call | solution.py:646
  237.3 2.3 shard_map.167

commit v5 on v4

--- a/solution.py
+++ b/solution.py
@@ -15,8 +15,8 @@
 MESH = pl.DeviceIdType.MESH
 
 N_CHUNK = 4
-N_A = 5
-N_B = 5
+N_A = 6
+N_B = 4
 GROUP = 16
 
 
@@ -71,6 +71,9 @@
             src_ref=src, dst_ref=dst, send_sem=send, recv_sem=recv,
             device_id={'pp': to_stage, 'tp': to_line}, device_id_type=MESH)
 
+    def stream(c):
+        return hb.at[c, :, pl.ds(N_A * sub, N_B * sub)]
+
     def landed(ref, sem):
         pltpu.make_async_copy(ref, ref, sem).wait()
 
@@ -99,7 +102,7 @@
         pltpu.make_async_copy(w_d.at[pl.ds(o_rows, w_d.shape[0] - o_rows)], wd.at[pl.ds(o_rows, w_d.shape[0] - o_rows)], s_w.at[6]),
         pltpu.make_async_copy(w_d.at[pl.ds(0, o_rows)], wd.at[pl.ds(0, o_rows)], s_w.at[7]),
     ]
-    for one in loads[:3]:
+    for one in loads[1:3] + loads[:1]:
         one.start()
     for one in load_kv(0, 0):
         one.start()
@@ -138,39 +141,35 @@
             @pl.when(is_end)
             def _():
                 for s in range(N_B):
-                    remote(part.at[kc, N_A + s], rec_m.at[k, s], s_part.at[kc, N_A + s], r_hm.at[k, s], helped, line).start()
+                    remote(part.at[kc, N_A + s], rec_m.at[k, s], s_part.at[kc], r_hm.at[k, s], helped, line).start()
 
             @pl.when(is_mid)
             def _():
                 for s in range(N_B):
-                    remote(part.at[kc, N_A + s], hrec1.at[kc, s], s_part.at[kc, N_A + s], r_h1.at[kc, s], helped, line).start()
+                    remote(part.at[kc, N_A + s], hrec1.at[kc, s], s_part.at[kc], r_h1.at[kc, s], helped, line).start()
         else:
             @pl.when(is_end)
             def _():
                 for s in range(N_A):
-                    remote(part.at[kc, s], rec_e.at[kc, s], s_part.at[kc, s], r_e.at[kc, s], stage, mid_of).start()
+                    remote(part.at[kc, s], rec_e.at[kc, s], s_part.at[kc], r_e.at[kc, s], stage, mid_of).start()
 
     def wait_part_sends(k):
         kc = lax.rem(k, N_CHUNK)
-        for s in range(N_B):
-            landed(part.at[kc, N_A + s], s_part.at[kc, N_A + s])
-
         @pl.when(is_end)
         def _():
-            for s in range(N_A):
-                landed(part.at[kc, s], s_part.at[kc, s])
+            landed(part.at[kc], s_part.at[kc])
 
         @pl.when(is_mid)
         def _():
-            for s in range(N_A):
-                landed(part.at[kc, s], s_sum.at[kc, s])
+            landed(part.at[kc, pl.ds(N_A, N_B)], s_part.at[kc])
+            landed(part.at[kc, pl.ds(0, N_A)], s_sum.at[kc])
 
     def sum_first(k):
         kc = lax.rem(k, N_CHUNK)
         for s in range(N_A):
             landed(rec_e.at[kc, s], r_e.at[kc, s])
             part[kc, s] = part[kc, s] + rec_e[kc, s]
-            remote(part.at[kc, s], rec_m.at[k, s], s_sum.at[kc, s], r_m.at[k, s], stage, other_mid).start()
+            remote(part.at[kc, s], rec_m.at[k, s], s_sum.at[kc], r_m.at[k, s], stage, other_mid).start()
 
     def sum_second(k):
         kc = lax.rem(k, N_CHUNK)
@@ -178,21 +177,22 @@
 
         @pl.when(k >= N_CHUNK)
         def _():
-            for s in range(N_A):
-                landed(res_a.at[kc, s], s_res.at[kc, s])
+            landed(res_a.at[kc], s_res.at[kc])
 
         for s in range(N_A):
             landed(rec_m.at[k, s], r_m.at[k, s])
-            res_a[k, s] = (part[kc, s] + rec_m[k, s]).astype(BF16)
-            remote(res_a.at[k, s], res_a.at[k, s], s_res.at[kc, s], r_a.at[k, s], to_stage, end_of).start()
+            summed = (part[kc, s] + rec_m[k, s]).astype(BF16)
+            carried = hb[kc, :, pl.ds(s * sub, sub)]
+            res_a[k, s] = jnp.where(k < N_CHUNK, summed, (carried.astype(F32) + summed.astype(F32)).astype(BF16))
+            remote(res_a.at[k, s], res_a.at[k, s], s_res.at[kc], r_a.at[k], to_stage, end_of).start()
 
             @pl.when(k >= N_CHUNK)
             def _():
-                remote(res_a.at[k, s], res_a.at[k, s], s_res2.at[kc, s], r_a.at[k, s], after, line).start()
+                remote(res_a.at[k, s], res_a.at[k, s], s_res2.at[kc], r_a.at[k], after, line).start()
 
             @pl.when(jnp.logical_and(k >= N_CHUNK, stage == last))
             def _():
-                remote(res_a.at[k, s], res_a.at[k, s], s_res3.at[kc, s], r_a.at[k, s], after, end_of).start()
+                remote(res_a.at[k, s], res_a.at[k, s], s_res3.at[kc], r_a.at[k], after, end_of).start()
 
     def help_first(k):
         kc = lax.rem(k, N_CHUNK)
@@ -200,7 +200,7 @@
             landed(hrec0.at[kc, s], r_h0.at[kc, s])
             landed(hrec1.at[kc, s], r_h1.at[kc, s])
             hrec1[kc, s] = hrec1[kc, s] + hrec0[kc, s]
-            remote(hrec1.at[kc, s], rec_m.at[k, s], s_hsum.at[kc, s], r_hm.at[k, s], stage, other_mid).start()
+            remote(hrec1.at[kc, s], rec_m.at[k, s], s_hsum.at[kc], r_hm.at[k, s], stage, other_mid).start()
 
     def help_second(k):
         kc = lax.rem(k, N_CHUNK)
@@ -208,33 +208,32 @@
 
         @pl.when(k >= N_CHUNK)
         def _():
-            for s in range(N_B):
-                landed(hres.at[kc, s], s_hres0.at[kc, s])
-                landed(hres.at[kc, s], s_hres1.at[kc, s])
+            landed(hres.at[kc], s_hres0.at[kc])
+            landed(hres.at[kc], s_hres1.at[kc])
 
         for s in range(N_B):
             landed(rec_m.at[k, s], r_hm.at[k, s])
-            landed(hrec1.at[kc, s], s_hsum.at[kc, s])
+            if s == 0:
+                landed(hrec1.at[kc], s_hsum.at[kc])
             hres[kc, s] = (hrec1[kc, s] + rec_m[k, s]).astype(BF16)
-            remote(hres.at[kc, s], res_b.at[k, s], s_hres0.at[kc, s], r_b.at[k, s], to_stage, end_of).start()
-            remote(hres.at[kc, s], res_b.at[k, s], s_hres1.at[kc, s], r_b.at[k, s], to_stage, line).start()
+            remote(hres.at[kc, s], res_b.at[k, s], s_hres0.at[kc], r_b.at[k], to_stage, end_of).start()
+            remote(hres.at[kc, s], res_b.at[k, s], s_hres1.at[kc], r_b.at[k], to_stage, line).start()
 
             @pl.when(jnp.logical_and(k >= N_CHUNK, stage == mirror))
             def _():
                 res_b[k, s] = hres[kc, s]
-                remote(hres.at[kc, s], res_b.at[k, s], s_hres2.at[kc, s], r_b.at[k, s], stage, end_of).start()
+                remote(hres.at[kc, s], res_b.at[k, s], s_hres2.at[kc], r_b.at[k], stage, end_of).start()
 
     def help_forward(k):
         kc = lax.rem(k, N_CHUNK)
 
         @pl.when(k >= N_CHUNK)
         def _():
-            for s in range(N_B):
-                landed(hrec0.at[kc, s], s_hsum.at[kc, s])
+            landed(hrec0.at[kc], s_hsum.at[kc])
 
         for s in range(N_B):
             landed(rec_m.at[k, s], r_hm.at[k, s])
-            remote(rec_m.at[k, s], hrec0.at[kc, s], s_hsum.at[kc, s], r_h0.at[kc, s], stage, mid_of).start()
+            remote(rec_m.at[k, s], hrec0.at[kc, s], s_hsum.at[kc], r_h0.at[kc, s], stage, mid_of).start()
 
     def help_stage(finish_early):
         @pl.when(is_end)
@@ -271,28 +270,31 @@
             def _():
                 sum_second(k - 2)
 
-    def add_sum(c, k, remote_a, remote_b=None):
+    def add_sum(c, k, remote_a, remote_b=None, whole_a=True):
         @pl.when(remote_a)
         def _():
-            for s in range(N_A):
-                landed(res_a.at[k, s], r_a.at[k, s])
+            landed(res_a.at[k], r_a.at[k])
 
         for s in range(N_A):
             at = pl.ds(s * sub, sub)
-            hb[c, :, at] = (hb[c, :, at].astype(F32) + res_a[k, s].astype(F32)).astype(BF16)
+            if whole_a:
+                hb[c, :, at] = res_a[k, s]
+            else:
+                hb[c, :, at] = (hb[c, :, at].astype(F32) + res_a[k, s].astype(F32)).astype(BF16)
+        if remote_b is None:
+            landed(res_b.at[k], r_b.at[k])
+        else:
+            @pl.when(remote_b)
+            def _():
+                landed(res_b.at[k], r_b.at[k])
+
         for s in range(N_B):
             at = pl.ds((N_A + s) * sub, sub)
-            if remote_b is None:
-                landed(res_b.at[k, s], r_b.at[k, s])
-            else:
-                @pl.when(remote_b)
-                def _():
-                    landed(res_b.at[k, s], r_b.at[k, s])
             hb[c, :, at] = (hb[c, :, at].astype(F32) + res_b[k, s].astype(F32)).astype(BF16)
 
     def partials(k, act, weight, depth):
         kc = lax.rem(k, N_CHUNK)
-        for b_half in (True, False):
+        for b_half in (False, True):
             base, count = (N_A, N_B) if b_half else (0, N_A)
             got = dot(act, weight[pl.ds(0, depth), pl.ds(base * sub, count * sub)])
             for s in range(count):
@@ -301,16 +303,14 @@
 
     def attention(c):
         slot = lax.rem(c, 2)
-        landed(hb.at[c], r_h.at[c])
+        @pl.when(stage == 0)
+        def _():
+            landed(hb.at[c], r_h.at[c])
 
         @pl.when(stage > 0)
         def _():
+            landed(stream(c), r_h.at[c])
             add_sum(c, N_CHUNK + c, stage > 0)
-
-        @pl.when(c == 0)
-        def _():
-            for one in loads[:3]:
-                one.wait()
 
         normed = norm_rows(hb[c], gain_a[...])
         base = pl.multiple_of(c * rows, rows)
@@ -322,6 +322,12 @@
             return (vals32 * cosv + pltpu.roll(vals32, head_dim // 2, 1) * sinv).astype(BF16)
 
         nb[...] = normed
+
+        @pl.when(c == 0)
+        def _():
+            for one in loads[1:3]:
+                one.wait()
+
         got_k = dot(nb[...], wk[...])
         got_v = dot(nb[...], wv[...])
         for g in range(kv_heads):
@@ -335,6 +341,11 @@
         vo[c] = mix[1].astype(BF16)
         pltpu.make_async_copy(ko.at[c], k_out.at[c], s_rows.at[0, c]).start()
         pltpu.make_async_copy(vo.at[c], v_out.at[c], s_rows.at[1, c]).start()
+
+        @pl.when(c == 0)
+        def _():
+            loads[0].wait()
+
         got_q = dot(nb[...], wq[...])
         for h in range(n_head):
             qb[:, pl.ds(h * head_dim, head_dim)] = rope(got_q[:, h * head_dim:(h + 1) * head_dim])
@@ -413,7 +424,7 @@
 
     def mlp_part(k):
         c = k - N_CHUNK
-        add_sum(c, c, is_end)
+        add_sum(c, c, is_end, whole_a=False)
         nb[...] = norm_rows(hb[c], gain_m[...])
 
         @pl.when(c == 0)
@@ -434,14 +445,14 @@
         wait_part_sends(k - N_CHUNK)
         partials(k, ab[...], wd, wd.shape[0])
 
-        remote(hb.at[c], hb.at[c], s_h.at[c], r_h.at[c], after, line).start()
+        remote(stream(c), stream(c), s_h.at[c], r_h.at[c], after, line).start()
 
     def finish(c, at_last):
         if at_last:
-            landed(hb.at[c], s_h.at[c])
+            landed(stream(c), s_h.at[c])
             add_sum(c, N_CHUNK + c, is_end)
         else:
-            landed(hb.at[c], r_h.at[c])
+            landed(stream(c), r_h.at[c])
             add_sum(c, N_CHUNK + c, stage == mirror, is_end)
         hb[c] = norm_rows(hb[c], gain_f[...].reshape(1, hb.shape[2]))
         remote(hb.at[c], out.at[c], s_fwd.at[c], r_out.at[c], stage - 1, line).start()
@@ -480,18 +491,16 @@
 
             @pl.when(stage < last)
             def _():
-                landed(hb.at[c], s_h.at[c])
+                landed(stream(c), s_h.at[c])
 
             @pl.when(is_mid)
             def _():
-                for s in range(N_A):
-                    landed(res_a.at[c, s], s_res.at[c, s])
-                    landed(res_a.at[c, s], s_res2.at[c, s])
+                landed(res_a.at[c], s_res.at[c])
+                landed(res_a.at[c], s_res2.at[c])
 
                 @pl.when(stage == last)
                 def _():
-                    for s in range(N_A):
-                        landed(res_a.at[c, s], s_res3.at[c, s])
+                    landed(res_a.at[c], s_res3.at[c])
 
     @pl.when(side == 1)
     def _():
@@ -512,19 +521,16 @@
     def _(c):
         @pl.when(is_mid)
         def _():
-            for s in range(N_B):
-                landed(hres.at[c, s], s_hres0.at[c, s])
-                landed(hres.at[c, s], s_hres1.at[c, s])
+            landed(hres.at[c], s_hres0.at[c])
+            landed(hres.at[c], s_hres1.at[c])
 
             @pl.when(stage == mirror)
             def _():
-                for s in range(N_B):
-                    landed(hres.at[c, s], s_hres2.at[c, s])
+                landed(hres.at[c], s_hres2.at[c])
 
         @pl.when(is_end)
         def _():
-            for s in range(N_B):
-                landed(hrec0.at[c, s], s_hsum.at[c, s])
+            landed(hrec0.at[c], s_hsum.at[c])
 
         spreads = jnp.logical_or(stage == last, stage == mirror)
 
@@ -637,9 +643,9 @@
                 pltpu.VMEM(b_blocks + tile, BF16),
                 dma((8,)), dma((2, 2)), dma((2, N_CHUNK)), dma((N_CHUNK,)), dma((N_CHUNK,)),
                 dma((N_CHUNK,)), dma((N_CHUNK,)), dma((N_CHUNK,)),
-                dma((N_CHUNK, N_A + N_B)), dma(a_blocks), dma(a_blocks), dma(a_blocks), dma(a_blocks),
-                dma(a_blocks), dma((2 * N_CHUNK, N_A)), dma((2 * N_CHUNK, N_A)), dma((2 * N_CHUNK, N_B)),
-                dma(b_blocks), dma(b_blocks), dma(b_blocks), dma(b_blocks), dma(b_blocks), dma(b_blocks), dma((2 * N_CHUNK, N_B)),
+                dma((N_CHUNK,)), dma((N_CHUNK,)), dma((N_CHUNK,)), dma((N_CHUNK,)), dma((N_CHUNK,)),
+                dma(a_blocks), dma((2 * N_CHUNK, N_A)), dma((2 * N_CHUNK,)), dma((2 * N_CHUNK,)),
+                dma((N_CHUNK,)), dma((N_CHUNK,)), dma((N_CHUNK,)), dma((N_CHUNK,)), dma(b_blocks), dma(b_blocks), dma((2 * N_CHUNK, N_B)),
             ],
             compiler_params=pltpu.CompilerParams(collective_id=0, has_side_effects=True, vmem_limit_bytes=67043328),
         )

time: 240 us -> 233 us (0.971)
  Pallas kernels: 239 us -> 232 us
    pallas_call x1, Pallas kernels: 237 us -> 230 us  [stage_fn(): call(hidden_in.reshape(N_CHUNK, rows, d_model), positions.reshape(-1, 128...]
where the time goes in v5:
time: 233 us
  Pallas kernels  232 us (100%)
    pallas_call x1, Pallas kernels, stage_fn(): call(hidden_in.reshape(N_CHUNK, rows, d_model), positions.reshape(-1, 128...  230 us

profile of v5, /device:TPU:0, one launch (start us, length us, event | category | flops | bytes accessed | tf_op | source)
XLA Modules:
  0.0 232.8 jit_solution(2669796243207320335)
XLA Ops:
  0.6 229.8 %shard_map.166 = (bf16[4,64,2560]{2,1,0:T(8,128)(2,1)}, bf16[4,128,128]{2,1,0:T(8,128)(2,1)}, bf16[4,128,128]{2,1,0:T(8,128)(2,1)}) custom-call(bf16[4,64,2560]{2,1,0:T(8,128)(2,1)} %bitcast.21, s32[2,128]{1,0:T(2,128)} %bitcast.24, f32[1,128]{1,0:T(1,128)} %constant.2.clone.inv_freq, bf16[4,4096,128]{2,1,0:T(8,128)(2,1)} %bitcast.19, ...), custom_call_target="tpu_custom_call" | custom-call | tf_op jit(solution)/shard_map/pallas_call | solution.py:652
  230.4 2.3 shard_map.167

commit v6 on v5

--- a/solution.py
+++ b/solution.py
@@ -442,6 +442,10 @@
             for one in loads[6:]:
                 one.wait()
 
+        @pl.when(k >= 2 * N_CHUNK - 2)
+        def _():
+            relay(k)
+
         wait_part_sends(k - N_CHUNK)
         partials(k, ab[...], wd, wd.shape[0])
 
@@ -472,7 +476,10 @@
         @pl.loop(N_CHUNK, 2 * N_CHUNK)
         def _(k):
             mlp_part(k)
-            relay(k)
+
+            @pl.when(k < 2 * N_CHUNK - 2)
+            def _():
+                relay(k)
 
         @pl.loop(2 * N_CHUNK, 3 * N_CHUNK)
         def _(k):

time: 233 us -> 231 us (level)
  no operation moved by 1% of the time
where the time goes in v6:
time: 231 us
  Pallas kernels  230 us (100%)
    pallas_call x1, Pallas kernels, stage_fn(): call(hidden_in.reshape(N_CHUNK, rows, d_model), positions.reshape(-1, 128...  228 us

profile of v6, /device:TPU:0, one launch (start us, length us, event | category | flops | bytes accessed | tf_op | source)
XLA Modules:
  0.0 231.1 jit_solution(14082606340033627548)
XLA Ops:
  0.6 228.1 %shard_map.166 = (bf16[4,64,2560]{2,1,0:T(8,128)(2,1)}, bf16[4,128,128]{2,1,0:T(8,128)(2,1)}, bf16[4,128,128]{2,1,0:T(8,128)(2,1)}) custom-call(bf16[4,64,2560]{2,1,0:T(8,128)(2,1)} %bitcast.21, s32[2,128]{1,0:T(2,128)} %bitcast.24, f32[1,128]{1,0:T(1,128)} %constant.2.clone.inv_freq, bf16[4,4096,128]{2,1,0:T(8,128)(2,1)} %bitcast.19, ...), custom_call_target="tpu_custom_call" | custom-call | tf_op jit(solution)/shard_map/pallas_call | solution.py:659
  228.8 2.3 %shard_map.167 = (bf16[4,64,2560]{2,1,0:T(8,128)(2,1)}, bf16[4,128,128]{2,1,0:T(8,128)(2,1)}, bf16[4,128,128]{2,1,0:T(8,128)(2,1)}) custom-call(bf16[4,64,2560]{2,1,0:T(8,128)(2,1)} %get-tuple-element.9.refs_0_, bf16[4,128,128]{2,1,0:T(8,128)(2,1)} %get-tuple-element.10.refs_1_, bf16[4,128,128]{2,1,0:T(8,128)(2,1)} %get-tuple-element.11.refs_2_), custom_call_target="tpu_custom_call" | custom-call | tf_op jit(solution)/shard_map/pallas_call | solution.py:574
